TPU v7x, 256 devices: a whole 4x4x8 slice. The times are simulated.
256 devices in a mesh: tm: 32 (over z, y), coef: 8 (over x, core).
Axes of the slice: x: 4, y: 4, z: 8, core: 2. Of those that a mesh axis runs over, the one named last changes fastest.
Arguments:
- design: bfloat16 [8192, 50176], P('tm', 'coef'), may hold values from -0.0546875 to 0.0546875
- observed: float32 [8192, 128], P('tm'), may hold values from -6 to 6
- slab_counts: int32 [32], P('tm'), may hold values from 128 to 256, as said below
- gap_mask: int32 [8192], P('tm'), may hold values 0 or 1
- filter_taps: float32 [128], replicated, may hold values from -0.5 to 1.2, as said below
- kaula_diag: float32 [50176], P('coef'), may hold values from 0.1 to 1
- precond: float32 [50176], P('coef'), may hold values from 0.3 to 3
Outputs:
- solution: float32 [50176, 128], P(('coef', 'tm'))
- residual: float32 [50176, 128], P(('coef', 'tm'))
Inputs may be any that keep to these rules, and one draw needn't show every extreme that they name: `slab_counts`: every slab holds at most 256 valid epochs, and some slab holds exactly 256. filter_taps[0] lies between 1 and 1.2.
All inputs are finite; a program needn't handle non-finite values. No bound on the sum of `gap_mask` on one device may be relied on, other than what follows from the above.
Results may differ from a plain program's by a relative error of at most 0.0065.
The roundings to bfloat16 on the way count: a program that leaves them out, or rounds other values in their place, can miss the bound.
Values may be sent and summed in bfloat16 or wider, within the bound.
A program may use at most 64 MiB of HBM per device.

v0:
```python
import functools

import jax
import jax.numpy as jnp
from jax import lax
from jax.sharding import Mesh
from jax.sharding import PartitionSpec as P

ITERS = 2
TM = ("tm_0", "tm_1")
TM_COEF = ("tm_0", "tm_1", "coef_0", "coef_1")
COEF = ("coef_0", "coef_1")
COEF_TM = ("coef_0", "coef_1", "tm_0", "tm_1")


def shifted(value, axis, steps):
    count = lax.axis_size(axis)
    first, last = (max(0, -steps), min(count, count - steps))
    return lax.ppermute(value, axis, [(source, source + steps) for source in range(first, last)])


def split_up(array, dim, count):
    dims = array.shape
    tiles = array.reshape(*dims[:dim], count, dims[dim] // count, *dims[dim + 1 :])
    return jnp.moveaxis(tiles, dim, 0)


def summed_on_arrival(array, axis, dim):
    count = lax.axis_size(axis)
    tiles = lax.all_to_all(split_up(array, dim, count), axis, 0, 0, tiled=True)
    return jnp.sum(tiles, axis=0)


def from_everyone(array, axis):
    copies = jnp.broadcast_to(array, (lax.axis_size(axis), *array.shape))
    return lax.all_to_all(copies, axis, split_axis=0, concat_axis=0, tiled=True)


def joined_along(tiles, dim):
    dims = list(tiles.shape[1:])
    dims[dim] *= tiles.shape[0]
    return jnp.moveaxis(tiles, 0, dim).reshape(dims)


def collect(array, axis, dim):
    tiles = from_everyone(array, axis)
    return joined_along(tiles, dim)


def one_axis_at_a_time(array, axes):
    return functools.reduce(lax.psum, axes, array)


def over_copies(array, axis):
    return from_everyone(array, axis).sum(axis=0)


def toeplitz(pattern, band_len):
    tiled = jnp.tile(pattern, band_len)[: band_len * (2 * band_len - 1)]
    return tiled.reshape(band_len, 2 * band_len - 1)[:, :band_len]


def block_pair(filter_taps):
    band_len = filter_taps.shape[0]
    spacer = jnp.zeros((band_len,), jnp.float32)
    reversed_taps = filter_taps[:0:-1]
    lower = jnp.concatenate([filter_taps[:1], spacer, reversed_taps])
    upper = jnp.concatenate([jnp.zeros((1,), jnp.float32), reversed_taps, spacer])
    return (toeplitz(lower, band_len), toeplitz(upper, band_len))


def forward(values, lower_block, upper_block):
    band_len = lower_block.shape[0]
    blocks = values.reshape(-1, band_len, values.shape[1])
    tail_block = shifted(blocks[-1], TM, 1)
    previous = jnp.concatenate([tail_block[None], blocks[:-1]], 0)
    result = jnp.einsum("ij,bjr->bir", lower_block, blocks, precision=lax.Precision.HIGHEST)
    result = result + jnp.einsum(
        "ij,bjr->bir", upper_block, previous, precision=lax.Precision.HIGHEST
    )
    return result.reshape(values.shape)


def backward(values, lower_block, upper_block):
    band_len = lower_block.shape[0]
    blocks = values.reshape(-1, band_len, values.shape[1])
    head_block = shifted(blocks[0], TM, -1)
    following = jnp.concatenate([blocks[1:], head_block[None]], 0)
    result = jnp.einsum("ji,bjr->bir", lower_block, blocks, precision=lax.Precision.HIGHEST)
    result = result + jnp.einsum(
        "ji,bjr->bir", upper_block, following, precision=lax.Precision.HIGHEST
    )
    return result.reshape(values.shape)


def shards(design, observed, slab_counts, gap_mask, filter_taps, kaula_diag, precond):
    epoch_rows, coef_rows = design.shape
    owned_rows = coef_rows // lax.axis_size(TM)
    owner_index = lax.axis_index(TM)
    lower_block, upper_block = block_pair(filter_taps)
    position = jnp.arange(epoch_rows, dtype=jnp.int32)
    weight = ((gap_mask == 1) & (position < slab_counts[0])).astype(jnp.float32)[:, None]

    def weighted(values):
        inner = forward(weight * values, lower_block, upper_block)
        return (weight * backward(inner, lower_block, upper_block)).astype(jnp.bfloat16)

    def transposed_term(filtered):
        return lax.dot_general(
            design, filtered, (((0,), (0,)), ((), ())), preferred_element_type=jnp.float32
        )

    def collect_rows(filtered):
        return summed_on_arrival(transposed_term(filtered), TM, 0)

    def global_sum(terms):
        return jax.tree.map(lambda part: one_axis_at_a_time(part, TM_COEF), terms)

    kaula_col = lax.dynamic_slice_in_dim(kaula_diag, owner_index * owned_rows, owned_rows, 0)[
        :, None
    ]
    precond_col = lax.dynamic_slice_in_dim(precond, owner_index * owned_rows, owned_rows, 0)[
        :, None
    ]
    residual = collect_rows(weighted(observed))
    solution = jnp.zeros_like(residual)
    scaled = precond_col * residual
    direction = scaled
    norm_now = global_sum(jnp.sum(residual * scaled, 0))
    for iteration in range(ITERS):
        slab_values = over_copies(
            jnp.dot(
                design,
                collect(direction.astype(jnp.bfloat16), TM, 0),
                preferred_element_type=jnp.float32,
            ),
            COEF,
        )
        image = collect_rows(weighted(slab_values)) + kaula_col * direction
        curvature, cross_term, image_norm = global_sum(
            (
                jnp.sum(direction * image, 0),
                jnp.sum(image * scaled, 0),
                jnp.sum(image * precond_col * image, 0),
            )
        )
        step_len = norm_now / curvature
        solution = solution + step_len * direction
        residual = residual - step_len * image
        if iteration + 1 < ITERS:
            scaled = precond_col * residual
            norm_next = norm_now - 2.0 * step_len * cross_term + step_len * step_len * image_norm
            direction = scaled + norm_next / norm_now * direction
            norm_now = norm_next
    return (solution, residual)


def solution(mesh):
    torus = Mesh(mesh.devices.reshape(8, 4, 4, 2), ("tm_0", "tm_1", "coef_0", "coef_1"))
    in_specs = (P(TM, COEF), P(TM, None), P(TM), P(TM), P(), P(COEF), P(COEF))
    out_specs = (P(COEF_TM, None), P(COEF_TM, None))
    return jax.shard_map(
        shards, mesh=torus, in_specs=in_specs, out_specs=out_specs, check_vma=False
    )
```

profile of v0, /device:TPU:1, one launch (start us, length us, event | category | flops | bytes accessed | tf_op | source)
XLA Modules:
  0.0 595.6 jit_solution(16350617517735958952)
XLA Ops:
  1.4 1.2 copy.54
  4.0 4.6 collective-permute-start
  11.5 1.2 reshape.67
  13.7 1.6 copy.103
  15.3 1.2 reshape.68
  16.6 1.3 fusion.2
  17.9 1.3 collective-permute-start.1
  19.5 3.4 collective-permute-done.1
  23.8 1.6 copy.94
  25.5 3.2 convolution_bitcast_fusion.2
  28.7 4.9 copy.61
  33.5 4.1 reshape.70
  37.7 12.5 %all-to-all-start = ((f32[32,196,128]{2,1,0:T(8,128)}), f32[32,196,128]{2,1,0:T(8,128)}, u32[]{:S(2)}, u32[]{:S(2)}) async-start(f32[32,196,128]{2,1,0:T(8,128)} %reshape.70), calls=%async_computation | async-start | bytes 6553600 | tf_op jit(solution)/shard_map/all_to_all | solution.py:30
  51.0 71.7 %all-to-all-done = f32[32,196,128]{2,1,0:T(8,128)} async-done(((f32[32,196,128]{2,1,0:T(8,128)}), f32[32,196,128]{2,1,0:T(8,128)}, u32[]{:S(2)}, u32[]{:S(2)}) %all-to-all-start) | async-done | bytes 3211296 | tf_op jit(solution)/shard_map/all_to_all | solution.py:30
  122.7 2.1 reduce_sum.89
  125.1 44.4 %all_to_all.35 = bf16[32,196,128]{2,1,0:T(8,128)(2,1)} all-to-all(bf16[32,196,128]{2,1,0:T(8,128)(2,1)S(1)} %broadcast_in_dim.44), channel_id=1, replica_groups=mesh['tm_0'=8,'tm_1'=4,'coef_0'=4,'coef_1'=2] {'tm_0','tm_1'}, dimensions={0} | all-to-all | bytes 3211264 | tf_op jit(solution)/shard_map/all_to_all | solution.py:36
  169.4 3.4 reshape.71
  172.8 3.3 convolution_bitcast_fusion.4
  176.1 1.7 copy.62
  177.7 2.0 broadcast_in_dim.45
  179.7 9.4 %all-to-all-start.2 = ((f32[8,256,128]{2,1,0:T(8,128)}), f32[8,256,128]{2,1,0:T(8,128)}, u32[]{:S(2)}, u32[]{:S(2)}) async-start(f32[8,256,128]{2,1,0:T(8,128)} %broadcast_in_dim.45), calls=%async_computation.2 | async-start | bytes 2097152 | tf_op jit(solution)/shard_map/all_to_all | solution.py:36
  189.1 15.1 %all-to-all-done.2 = f32[8,256,128]{2,1,0:T(8,128)} async-done(((f32[8,256,128]{2,1,0:T(8,128)}), f32[8,256,128]{2,1,0:T(8,128)}, u32[]{:S(2)}, u32[]{:S(2)}) %all-to-all-start.2) | async-done | bytes 1048608 | tf_op jit(solution)/shard_map/all_to_all | solution.py:36
  204.2 1.9 reduce_sum.91
  206.1 1.7 copy.64
  207.7 1.6 copy.63
  210.3 2.4 collective-permute-start.2
  212.7 1.2 fusion.26
  214.3 1.3 collective-permute-start.3
  216.8 2.9 collective-permute-done.3
  220.6 1.6 copy.97
  222.3 3.2 convolution_bitcast_fusion.1
  225.4 4.9 copy.70
  230.3 4.1 reshape.73
  234.4 8.4 %all-to-all-start.3 = ((f32[32,196,128]{2,1,0:T(8,128)}), f32[32,196,128]{2,1,0:T(8,128)}, u32[]{:S(2)}, u32[]{:S(2)}) async-start(f32[32,196,128]{2,1,0:T(8,128)} %reshape.73), calls=%async_computation.3 | async-start | bytes 6553600 | tf_op jit(solution)/shard_map/all_to_all | solution.py:30
  242.8 1.3 dynamic_slice.7
  244.1 70.3 %all-to-all-done.3 = f32[32,196,128]{2,1,0:T(8,128)} async-done(((f32[32,196,128]{2,1,0:T(8,128)}), f32[32,196,128]{2,1,0:T(8,128)}, u32[]{:S(2)}, u32[]{:S(2)}) %all-to-all-start.3) | async-done | bytes 3211296 | tf_op jit(solution)/shard_map/all_to_all | solution.py:30
  314.5 2.1 reduce_sum.93
  316.6 1.3 fusion.30
  317.8 11.4 %all-reduce = (f32[128]{0:T(128)}, f32[128]{0:T(128)}, f32[128]{0:T(128)}) all-reduce(f32[128]{0:T(128)} %get-tuple-element.3, f32[128]{0:T(128)} %get-tuple-element.4, f32[128]{0:T(128)} %get-tuple-element.2), channel_id=1, replica_groups=mesh['tm_0'=8,'tm_1'=4,'coef_0'=4,'coef_1'=2] {'tm_0'}, use_global_device_ids=true, to_apply=%region_14.0 | all-reduce | flops 384 | bytes 3072 | tf_op jit(solution)/shard_map/psum | solution.py:51
  329.2 11.1 %all-reduce.2 = (f32[128]{0:T(128)}, f32[128]{0:T(128)}, f32[128]{0:T(128)}) all-reduce(f32[128]{0:T(128)} %get-tuple-element.5, f32[128]{0:T(128)} %get-tuple-element.6, f32[128]{0:T(128)} %get-tuple-element.7), channel_id=1, replica_groups=mesh['tm_0'=8,'tm_1'=4,'coef_0'=4,'coef_1'=2] {'tm_1'}, use_global_device_ids=true, to_apply=%region_15.0 | all-reduce | flops 384 | bytes 3072 | tf_op jit(solution)/shard_map/psum | solution.py:51
  340.3 7.6 %all-reduce.1 = (f32[128]{0:T(128)}, f32[128]{0:T(128)}, f32[128]{0:T(128)}) all-reduce(f32[128]{0:T(128)} %get-tuple-element.11, f32[128]{0:T(128)} %get-tuple-element.12, f32[128]{0:T(128)} %get-tuple-element.13), channel_id=1, replica_groups=mesh['tm_0'=8,'tm_1'=4,'coef_0'=4,'coef_1'=2] {'coef_0'}, use_global_device_ids=true, to_apply=%region_16.0 | all-reduce | flops 384 | bytes 3072 | tf_op jit(solution)/shard_map/psum | solution.py:51
  347.9 14.2 %all-reduce.3 = (f32[128]{0:T(128)}, f32[128]{0:T(128)}, f32[128]{0:T(128)}) all-reduce(f32[128]{0:T(128)} %get-tuple-element.8, f32[128]{0:T(128)} %get-tuple-element.9, f32[128]{0:T(128)} %get-tuple-element.10), channel_id=1, replica_groups=mesh['tm_0'=8,'tm_1'=4,'coef_0'=4,'coef_1'=2] {'coef_1'}, use_global_device_ids=true, to_apply=%region_17.0 | all-reduce | flops 384 | bytes 3072 | tf_op jit(solution)/shard_map/psum | solution.py:51
  362.1 1.2 fusion.49
  364.9 45.6 %all_to_all.36 = bf16[32,196,128]{2,1,0:T(8,128)(2,1)} all-to-all(bf16[32,196,128]{2,1,0:T(8,128)(2,1)S(1)} %broadcast_in_dim.48), channel_id=1, replica_groups=mesh['tm_0'=8,'tm_1'=4,'coef_0'=4,'coef_1'=2] {'tm_0','tm_1'}, dimensions={0} | all-to-all | bytes 3211264 | tf_op jit(solution)/shard_map/all_to_all | solution.py:36
  410.5 3.4 reshape.74
  413.8 3.2 convolution_bitcast_fusion.3
  417.1 1.7 copy.71
  419.7 20.2 %all_to_all.37 = f32[8,256,128]{2,1,0:T(8,128)} all-to-all(f32[8,256,128]{2,1,0:T(8,128)S(1)} %broadcast_in_dim.49), channel_id=1, replica_groups=mesh['tm_0'=8,'tm_1'=4,'coef_0'=4,'coef_1'=2] {'coef_0','coef_1'}, dimensions={0} | all-to-all | bytes 2097152 | tf_op jit(solution)/shard_map/all_to_all | solution.py:36
  439.9 1.9 reduce_sum.96
  441.8 1.6 copy.73
  445.0 3.3 collective-permute-start.4
  448.3 1.6 copy.72
  449.9 1.2 fusion.24
  452.3 1.3 collective-permute-start.5
  454.8 2.5 collective-permute-done.5
  459.3 2.3 convolution_bitcast_fusion
  461.6 4.9 copy.79
  466.5 4.1 reshape.76
  470.6 82.6 %all_to_all.38 = f32[32,196,128]{2,1,0:T(8,128)} all-to-all(f32[32,196,128]{2,1,0:T(8,128)} %reshape.76), channel_id=1, replica_groups=mesh['tm_0'=8,'tm_1'=4,'coef_0'=4,'coef_1'=2] {'tm_0','tm_1'}, dimensions={0} | all-to-all | bytes 6422528 | tf_op jit(solution)/shard_map/all_to_all | solution.py:30
  553.2 2.1 reduce_sum.98
  555.5 11.6 %psum.136 = f32[128]{0:T(128)S(1)} all-reduce(f32[128]{0:T(128)S(1)} %multiply_reduce_fusion), channel_id=1, replica_groups=mesh['tm_0'=8,'tm_1'=4,'coef_0'=4,'coef_1'=2] {'tm_0'}, use_global_device_ids=true, to_apply=%region_21.0 | all-reduce | flops 128 | bytes 1024 | tf_op jit(solution)/shard_map/psum | solution.py:51
  567.1 7.1 %psum.137 = f32[128]{0:T(128)S(1)} all-reduce(f32[128]{0:T(128)S(1)} %psum.136), channel_id=1, replica_groups=mesh['tm_0'=8,'tm_1'=4,'coef_0'=4,'coef_1'=2] {'tm_1'}, use_global_device_ids=true, to_apply=%region_22.0 | all-reduce | flops 128 | bytes 1024 | tf_op jit(solution)/shard_map/psum | solution.py:51
  574.2 6.8 %psum.138 = f32[128]{0:T(128)S(1)} all-reduce(f32[128]{0:T(128)S(1)} %psum.137), channel_id=1, replica_groups=mesh['tm_0'=8,'tm_1'=4,'coef_0'=4,'coef_1'=2] {'coef_0'}, use_global_device_ids=true, to_apply=%region_23.0 | all-reduce | flops 128 | bytes 1024 | tf_op jit(solution)/shard_map/psum | solution.py:51
  581.1 13.7 %psum.139 = f32[128]{0:T(128)S(1)} all-reduce(f32[128]{0:T(128)S(1)} %psum.138), channel_id=1, replica_groups=mesh['tm_0'=8,'tm_1'=4,'coef_0'=4,'coef_1'=2] {'coef_1'}, use_global_device_ids=true, to_apply=%region_24.0 | all-reduce | flops 128 | bytes 1024 | tf_op jit(solution)/shard_map/psum | solution.py:51
  (59 shorter events, 20.4 us)
Async XLA Ops:
  0.6 24.9 %copy-start = (bf16[256,6272]{1,0:T(8,128)(2,1)S(1)}, bf16[256,6272]{1,0:T(8,128)(2,1)}, u32[]{:S(2)}) copy-start(bf16[256,6272]{1,0:T(8,128)(2,1)} %param.7) | copy-start | bytes 9633796
  4.0 12.6 %collective-permute-start = (f32[128,128]{0,1:T(8,128)}, f32[128,128]{0,1:T(8,128)}, u32[]{:S(2)}, u32[]{:S(2)}) collective-permute-start(f32[128,128]{0,1:T(8,128)} %get-tuple-element.32), channel_id=1, source_target_pairs={{0,8},{8,16},{16,24},{24,32},{32,40},{40,48},{48,56},{56,64},{64,7... | collective-permute-start | bytes 196616 | tf_op jit(solution)/shard_map/ppermute | solution.py:19
  12.8 15.9 %copy-start.1 = (f32[128,255]{1,0:T(8,128)}, f32[128,255]{1,0:T(8,128)S(1)}, u32[]{:S(2)}) copy-start(f32[128,255]{1,0:T(8,128)S(1)} %reshape.67) | copy-start | bytes 391684
  17.9 5.0 collective-permute-start.1
  37.7 85.0 %all-to-all-start = ((f32[32,196,128]{2,1,0:T(8,128)}), f32[32,196,128]{2,1,0:T(8,128)}, u32[]{:S(2)}, u32[]{:S(2)}) async-start(f32[32,196,128]{2,1,0:T(8,128)} %reshape.70), calls=%async_computation | async-start | bytes 6553600 | tf_op jit(solution)/shard_map/all_to_all | solution.py:30
  172.8 16.3 %copy-start.8 = (s32[256]{0:T(256)S(1)}, s32[256]{0:T(256)}, u32[]{:S(2)}) copy-start(s32[256]{0:T(256)} %param.10) | copy-start | bytes 3076
  179.7 24.4 %all-to-all-start.2 = ((f32[8,256,128]{2,1,0:T(8,128)}), f32[8,256,128]{2,1,0:T(8,128)}, u32[]{:S(2)}, u32[]{:S(2)}) async-start(f32[8,256,128]{2,1,0:T(8,128)} %broadcast_in_dim.45), calls=%async_computation.2 | async-start | bytes 2097152 | tf_op jit(solution)/shard_map/all_to_all | solution.py:36
  189.1 36.3 %copy-start.3 = (f32[2,128]{1,0:T(2,128)}, f32[2,128]{1,0:T(2,128)S(1)}, u32[]{:S(2)}) copy-start(f32[2,128]{1,0:T(2,128)S(1)} %fusion.66) | copy-start | bytes 3076
  210.3 3.7 collective-permute-start.2
  214.3 5.3 collective-permute-start.3
  234.4 80.0 %all-to-all-start.3 = ((f32[32,196,128]{2,1,0:T(8,128)}), f32[32,196,128]{2,1,0:T(8,128)}, u32[]{:S(2)}, u32[]{:S(2)}) async-start(f32[32,196,128]{2,1,0:T(8,128)} %reshape.73), calls=%async_computation.3 | async-start | bytes 6553600 | tf_op jit(solution)/shard_map/all_to_all | solution.py:30
  363.3 0.6 copy-start.4
  363.3 0.6 copy-start.6
  445.0 6.1 %collective-permute-start.4 = (f32[128,128]{0,1:T(8,128)}, f32[128,128]{0,1:T(8,128)}, u32[]{:S(2)}, u32[]{:S(2)}) collective-permute-start(f32[128,128]{0,1:T(8,128)} %get-tuple-element.24), channel_id=1, source_target_pairs={{0,8},{8,16},{16,24},{24,32},{32,40},{40,48},{48,56},{56,64},{64,7... | collective-permute-start | bytes 196616 | tf_op jit(solution)/shard_map/ppermute | solution.py:19
  452.3 5.0 collective-permute-start.5
  553.2 2.1 copy-start.2
  553.2 2.1 copy-start.5
  553.2 2.1 copy-start.7
  553.2 41.6 %copy-start.9 = (f32[128]{0:T(128)S(1)}, f32[128]{0:T(128)}, u32[]{:S(2)}) copy-start(f32[128]{0:T(128)} %get-tuple-element.18) | copy-start | bytes 1540
where the time goes:
time: 598 us; the launch traced here: 596 us
  blocking collectives  276 us (46%)
  waiting for transfers between devices  166 us (28%)
  local copies, waits for them, and re-layouts  62.9 us (11%)
  starting transfers between devices  44.4 us (7%)
  matrix products  26.6 us (4%)
  other arithmetic  17.7 us (3%)
    all_to_all x2, waiting for transfers between devices, summed_on_arrival(): tiles = lax.all_to_all(split_up(array, dim, count), axis, 0, 0, tiled=True)  142 us
    all_to_all x3, blocking collectives, from_everyone(): return lax.all_to_all(copies, axis, split_axis=0, concat_axis=0, tiled=True)  110 us
    psum x8, blocking collectives, one_axis_at_a_time(): return functools.reduce(lax.psum, axes, array)  83.5 us
    all_to_all x1, blocking collectives, summed_on_arrival(): tiles = lax.all_to_all(split_up(array, dim, count), axis, 0, 0, tiled=True)  82.6 us
    all_to_all x2, starting transfers between devices, summed_on_arrival(): tiles = lax.all_to_all(split_up(array, dim, count), axis, 0, 0, tiled=True)  20.9 us
    all_to_all x1, waiting for transfers between devices, from_everyone(): return lax.all_to_all(copies, axis, split_axis=0, concat_axis=0, tiled=True)  15.1 us
    dot_general x3, local copies, waits for them, and re-layouts, transposed_term(): lax.dot_general(design, filtered, (((0,), (0,)), ((), ())), preferred_ele...  14.6 us
    ppermute x6, starting transfers between devices, shifted(): lax.ppermute(value, axis, [(source, source + steps) for source in range(f...  14.2 us
  transfers between devices with their start and end apart: 9, of which 7 were waited for; matrix products, arithmetic and copies ran while one was open for 3% of the time, Pallas kernels for 0%

commit v1 on v0

v1 whole, which is shorter than its diff:
```python
import functools

import jax
import jax.numpy as jnp
from jax import lax
from jax.experimental import pallas as pl
from jax.experimental.pallas import tpu as pltpu
from jax.sharding import Mesh
from jax.sharding import PartitionSpec as P

AXES = ("z", "y", "x", "c")
TM = ("z", "y")
COEF = ("x", "c")
MESH = pl.DeviceIdType.MESH
NZ, NY, NX, NC = 8, 4, 4, 2
NA, NB = 104, 92
RA, RB = 112, 96
BAND = 128
F32 = jnp.float32
BF16 = jnp.bfloat16
HIGH = lax.Precision.HIGHEST


def dot(a, b, precision=None):
    return jnp.dot(a, b, preferred_element_type=F32, precision=precision)


def rcopy(src, dst, ssem, rsem, **device):
    return pltpu.make_async_remote_copy(
        src_ref=src, dst_ref=dst, send_sem=ssem, recv_sem=rsem, device_id=device, device_id_type=MESH
    )


def kernel(
    aa, ab, ata, atb, obs, wm, lo, up, lot, upt, kda, kdb, pca, pcb,
    xout, rout,
    bm, y_a, y_b,
    sa, ra, sya, rya, sb, rb, szb, rzb,
    ga, gb, vs, vr, us, ur, hx, scs, scr, scc,
    sem_sa, sem_ra, sem_sya, sem_rya, sem_sb, sem_rb, sem_szb, sem_rzb,
    sem_gs, sem_ga, sem_gay, sem_gb, sem_gby,
    sem_vs, sem_vr, sem_us, sem_ur, sem_hs, sem_hr, sem_cs, sem_cr,
):
    z, y, x, c = (lax.axis_index(name) for name in AXES)
    t = z * NY + y
    zp = [lax.rem(z + k, NZ) for k in range(NZ)]
    zm = [lax.rem(z + NZ - k, NZ) for k in range(NZ)]
    yp = [lax.rem(y + k, NY) for k in range(NY)]
    ym = [lax.rem(y + NY - k, NY) for k in range(NY)]
    xp = [lax.rem(x + k, NX) for k in range(NX)]
    other = 1 - c
    t_up = lax.rem(t + 1, NZ * NY)
    t_down = lax.rem(t + NZ * NY - 1, NZ * NY)
    pending = []

    def send(src, dst, ssem, rsem, **device):
        copy = rcopy(src, dst, ssem, rsem, **device)
        copy.start()
        pending.append(copy)

    def arrived(dst, ssem, rsem, **device):
        rcopy(dst, dst, ssem, rsem, **device).wait_recv()

    barrier = pltpu.get_barrier_semaphore()
    peers = [dict(z=zp[k]) for k in range(1, NZ)] + [dict(y=yp[k]) for k in range(1, NY)]
    peers += [dict(x=xp[k]) for k in range(1, NX)] + [dict(c=other)]
    for step in (t_up, t_down):
        for core in range(NC):
            peers.append(dict(z=lax.div(step, NY), y=lax.rem(step, NY), c=jnp.int32(core)))
    for peer in peers:
        pl.semaphore_signal(barrier, inc=1, device_id=peer, device_id_type=MESH)

    keep_first = jnp.where(t == 0, 0.0, 1.0).astype(F32)
    keep_last = jnp.where(t == NZ * NY - 1, 0.0, 1.0).astype(F32)
    ll = dot(lot[...], lo[...], HIGH)
    uu = dot(upt[...], up[...], HIGH)
    lu = dot(lot[...], up[...], HIGH)
    ul = dot(upt[...], lo[...], HIGH)
    zero = jnp.zeros((BAND, BAND), F32)
    bm[0:BAND, 0:BAND] = keep_first * lu
    bm[0:BAND, BAND : 2 * BAND] = ll + uu
    bm[0:BAND, 2 * BAND : 3 * BAND] = ul
    bm[0:BAND, 3 * BAND :] = zero
    bm[BAND:, 0:BAND] = zero
    bm[BAND:, BAND : 2 * BAND] = lu
    bm[BAND:, 2 * BAND : 3 * BAND] = ll + keep_last * uu
    bm[BAND:, 3 * BAND :] = keep_last * ul

    def filtered(st):
        ext = hx[st].reshape(4 * BAND, BAND)
        return (wm[...] * dot(bm[...], ext, HIGH)).astype(BF16)

    def small_start(i, block):
        scs[i, 0] = block
        for k in range(1, NY):
            send(scs.at[i, 0], scr.at[i, k], sem_cs.at[i, k], sem_cr.at[i, k], y=yp[k])

    def small_middle(i):
        total = scs[i, 0]
        for k in range(1, NY):
            arrived(scr.at[i, k], sem_cs.at[i, k], sem_cr.at[i, k], y=yp[k])
            total = total + scr[i, k]
        scs[i, 1] = total
        for k in range(1, NZ):
            send(scs.at[i, 1], scr.at[i, NY + k], sem_cs.at[i, NY + k], sem_cr.at[i, NY + k], z=zp[k])

    def small_end(i):
        total = scs[i, 1]
        for k in range(1, NZ):
            arrived(scr.at[i, NY + k], sem_cs.at[i, NY + k], sem_cr.at[i, NY + k], z=zp[k])
            total = total + scr[i, NY + k]
        return total

    half = NZ // 2 * RB

    def scatter(st, w, early, late):
        part = dot(atb[yp[2]], w).reshape(2, NZ // 2, RB, 128)
        for way, peer in ((0, yp[1]), (1, ym[1])):
            sb[st, way, 0] = part[way]
            send(sb.at[st, way, 0], rb.at[st, way, 0], sem_sb.at[st, way, 0], sem_rb.at[st, way, 0], y=peer)
        for way, target, peer in ((0, zp[4], zp[1]), (1, zm[3], zm[1])):
            sa[st, way, 0] = dot(ata[target], w).reshape(NY, RA, 128)
            for j in range(NY):
                send(
                    sa.at[st, way, 0, j], ra.at[st, way, 0, j],
                    sem_sa.at[st, way, 0, j], sem_ra.at[st, way, 0, j], z=peer,
                )
        for way, peer in ((0, yp[1]), (1, ym[1])):
            part = dot(atb[peer], w).reshape(2, NZ // 2, RB, 128)
            sb[st, way, 1] = part[1 - way]
            send(sb.at[st, way, 1], rb.at[st, way, 1], sem_sb.at[st, way, 1], sem_rb.at[st, way, 1], y=peer)
            sb[st, way, 2] = part[way]

        def product(i, carry):
            target = lax.rem(z + 5 + jnp.where(i < 3, 0, 0) + i, NZ)
            y_a[target] = dot(ata[target], w).reshape(NY, RA, 128)
            return carry

        lax.fori_loop(1, NZ - 1, product, 0)
        y_b[...] = dot(atb[y], w).reshape(NZ, RB, 128)
        early()
        for s in range(1, 4):
            for j in range(NY):
                for way, target, peer in ((0, zp[4 - s], zp[1]), (1, zm[3 - s], zm[1])):
                    if way == 1 and s == 3:
                        continue
                    arrived(
                        ra.at[st, way, s - 1, j], sem_sa.at[st, way, s - 1, j], sem_ra.at[st, way, s - 1, j], z=peer
                    )
                    sa[st, way, s, j] = ra[st, way, s - 1, j] + y_a[target, j]
                    send(
                        sa.at[st, way, s, j], ra.at[st, way, s, j],
                        sem_sa.at[st, way, s, j], sem_ra.at[st, way, s, j], z=peer,
                    )
            if s == 1:
                for way, peer in ((0, yp[1]), (1, ym[1])):
                    arrived(rb.at[st, way, 0], sem_sb.at[st, way, 0], sem_rb.at[st, way, 0], y=peer)
                    sb[st, way, 2] = sb[st, way, 2] + rb[st, way, 0]
                    send(
                        sb.at[st, way, 2], rb.at[st, way, 2], sem_sb.at[st, way, 2], sem_rb.at[st, way, 2], y=peer
                    )
                late()
            if s == 2:
                for way, peer in ((0, yp[1]), (1, ym[1])):
                    for kind in (1, 2):
                        arrived(
                            rb.at[st, way, kind], sem_sb.at[st, way, kind], sem_rb.at[st, way, kind], y=peer
                        )
                szb[st, 0 : NZ // 2] = y_b[0 : NZ // 2] + rb[st, 0, 2] + rb[st, 1, 1]
                szb[st, NZ // 2 :] = y_b[NZ // 2 :] + rb[st, 0, 1] + rb[st, 1, 2]
                for k in (4, 3, 5, 2, 6, 1, 7):
                    send(szb.at[st, zp[k]], rzb.at[st, k], sem_szb.at[st, k], sem_rzb.at[st, k], z=zp[k])
        for j in range(NY):
            arrived(ra.at[st, 0, 3, j], sem_sa.at[st, 0, 3, j], sem_ra.at[st, 0, 3, j], z=zp[1])
            arrived(ra.at[st, 1, 2, j], sem_sa.at[st, 1, 2, j], sem_ra.at[st, 1, 2, j], z=zm[1])
            sya[st, j] = ra[st, 0, 3, j] + ra[st, 1, 2, j] + y_a[z, j]
        for k in (2, 1, 3):
            send(sya.at[st, yp[k]], rya.at[st, k], sem_sya.at[st, k], sem_rya.at[st, k], y=yp[k])
        sum_b = szb[st, z]
        for k in range(1, NZ):
            arrived(rzb.at[st, k], sem_szb.at[st, k], sem_rzb.at[st, k], z=zp[k])
            sum_b = sum_b + rzb[st, k]
        sum_a = sya[st, y]
        for k in range(1, NY):
            arrived(rya.at[st, k], sem_sya.at[st, k], sem_rya.at[st, k], y=yp[k])
            sum_a = sum_a + rya[st, k]
        return sum_a, sum_b

    first_half, second_half = (0, 1, 7, 2), (6, 3, 5, 4)

    def gathered_product(it, rows_a, rows_b, middle):
        ga[it, z, y] = rows_a.astype(BF16)
        gb[it, y, z] = rows_b.astype(BF16)

        def put_a(way, s, k):
            zz, yy = (zm[s] if way == 0 else zp[s]), ym[k]
            peer = zp[1] if way == 0 else zm[1]
            send(ga.at[it, zz, yy], ga.at[it, zz, yy], sem_gs.at[it, 0, way, s, k], sem_ga.at[it, way, s, k], z=peer)

        def got_a(way, s, k):
            zz, yy = (zm[s + 1] if way == 0 else zp[s + 1]), ym[k]
            arrived(ga.at[it, zz, yy], sem_gs.at[it, 0, way, s, k], sem_ga.at[it, way, s, k], z=zp[1])

        def put_b(way, s, k):
            zz, yy = zm[k], (ym[s] if way == 0 else yp[s])
            peer = yp[1] if way == 0 else ym[1]
            send(gb.at[it, yy, zz], gb.at[it, yy, zz], sem_gs.at[it, 1, way, s, k], sem_gby.at[it, way, s, k], y=peer)

        def got_b(way, s, k):
            zz, yy = zm[k], (ym[s + 1] if way == 0 else yp[s + 1])
            arrived(gb.at[it, yy, zz], sem_gs.at[it, 1, way, s, k], sem_gby.at[it, way, s, k], y=yp[1])

        for k in (2, 1, 3):
            send(ga.at[it, z, y], ga.at[it, z, y], sem_gs.at[it, 0, 0, 4, k], sem_gay.at[it, k], y=yp[k])
        put_a(0, 0, 0)
        put_a(1, 0, 0)
        for k in (4, 3, 5, 2, 6, 1, 7):
            send(gb.at[it, y, z], gb.at[it, y, z], sem_gs.at[it, 1, 0, 2, k], sem_gb.at[it, k], z=zp[k])
        put_b(0, 0, 0)
        put_b(1, 0, 0)
        for k in (1, 3, 2):
            arrived(ga.at[it, z, ym[k]], sem_gs.at[it, 0, 0, 4, k], sem_gay.at[it, k], y=yp[k])
            put_a(0, 0, k)
            put_a(1, 0, k)
        v = dot(aa[z], ga[it, z].reshape(NY * RA, 128))
        for s in range(1, 4):
            for k in (0, 1, 3, 2):
                got_a(0, s - 1, k)
                put_a(0, s, k)
                got_a(1, s - 1, k)
                if s < 3:
                    put_a(1, s, k)
            if s == 1:
                for k in (1, 7, 2, 6, 3, 5, 4):
                    arrived(gb.at[it, y, zm[k]], sem_gs.at[it, 1, 0, 2, k], sem_gb.at[it, k], z=zp[k])
                    put_b(0, 0, k)
                    put_b(1, 0, k)
            if s == 2:
                for k in first_half:
                    got_b(0, 0, k)
                    put_b(0, 1, k)
                for k in second_half:
                    got_b(1, 0, k)
                    put_b(1, 1, k)
                middle()
            v = v + dot(aa[zm[s]], ga[it, zm[s]].reshape(NY * RA, 128))
            v = v + dot(aa[zp[s]], ga[it, zp[s]].reshape(NY * RA, 128))
        v = v + dot(ab[y], gb[it, y].reshape(NZ * RB, 128))
        for k in second_half:
            got_b(0, 0, k)
        for k in first_half:
            got_b(1, 0, k)
        v = v + dot(ab[yp[1]], gb[it, yp[1]].reshape(NZ * RB, 128))
        v = v + dot(ab[ym[1]], gb[it, ym[1]].reshape(NZ * RB, 128))
        for k in first_half:
            got_b(0, 1, k)
        for k in second_half:
            got_b(1, 1, k)
        v = v + dot(ab[yp[2]], gb[it, yp[2]].reshape(NZ * RB, 128))
        for k in range(NY):
            got_a(0, 3, k)
        return v + dot(aa[zm[4]], ga[it, zm[4]].reshape(NY * RA, 128))

    def slab_values(it, v, scal, finish):
        vs[it] = v.reshape(2, BAND, 128)
        scc[it, 0] = scal
        send(vs.at[it, other], vr.at[it], sem_vs.at[it, 0], sem_vr.at[it, 0], c=other)
        send(scc.at[it, 0], scc.at[it, 1], sem_vs.at[it, 1], sem_vr.at[it, 1], c=other)
        arrived(vr.at[it], sem_vs.at[it, 0], sem_vr.at[it, 0], c=other)
        arrived(scc.at[it, 1], sem_vs.at[it, 1], sem_vr.at[it, 1], c=other)
        us[it, 0:BAND] = vs[it, c] + vr[it]
        us[it, BAND:] = scc[it, 0] + scc[it, 1]
        for k in (2, 1, 3):
            send(us.at[it], ur.at[it, k], sem_us.at[it, k], sem_ur.at[it, k], x=xp[k])
        total = us[it]
        for k in range(1, NX):
            arrived(ur.at[it, k], sem_us.at[it, k], sem_ur.at[it, k], x=xp[k])
            total = total + ur[it, k]
        mask = wm[pl.ds(pl.multiple_of(c * BAND, BAND), BAND), :]
        block, scal = finish(mask * total[0:BAND], total[BAND:])
        hx[it + 1, 1 + c] = block
        slot = 3 - 3 * c
        step = jnp.where(c == 0, t_down, t_up)
        mine = hx.at[it + 1, 1 + c]
        send(mine, mine, sem_hs.at[it + 1, 1 + c], sem_hr.at[it + 1, 1 + c], c=other)
        for core in range(NC):
            send(
                mine, hx.at[it + 1, slot], sem_hs.at[it + 1, 4 + core], sem_hr.at[it + 1, slot],
                z=lax.div(step, NY), y=lax.rem(step, NY), c=jnp.int32(core),
            )
        for place in (2 - c, 0, 3):
            arrived(hx.at[it + 1, place], sem_hs.at[it + 1, 0], sem_hr.at[it + 1, place], c=other)
        return block, scal

    masked = wm[...] * obs[...]
    hx[0, 1] = masked[0:BAND]
    hx[0, 2] = masked[BAND:]
    pl.semaphore_wait(barrier, len(peers))
    send(
        hx.at[0, 2], hx.at[0, 0], sem_hs.at[0, 0], sem_hr.at[0, 0],
        z=lax.div(t_up, NY), y=lax.rem(t_up, NY),
    )
    send(
        hx.at[0, 1], hx.at[0, 3], sem_hs.at[0, 3], sem_hr.at[0, 3],
        z=lax.div(t_down, NY), y=lax.rem(t_down, NY),
    )
    arrived(hx.at[0, 0], sem_hs.at[0, 0], sem_hr.at[0, 0], c=other)
    arrived(hx.at[0, 3], sem_hs.at[0, 3], sem_hr.at[0, 3], c=other)
    nothing = lambda: None
    res_a, res_b = scatter(0, filtered(0), nothing, nothing)

    def col_sum(a, b):
        return jnp.sum(a, 0, keepdims=True) + jnp.sum(b, 0, keepdims=True)

    def rows_of(*rows):
        spare = jnp.zeros((8 - len(rows), 128), F32)
        return jnp.concatenate([*rows, spare], 0)

    dir_a, dir_b = pca[...] * res_a, pcb[...] * res_b
    small_start(0, rows_of(col_sum(res_a * dir_a, res_b * dir_b), col_sum(kda[...] * dir_a * dir_a, kdb[...] * dir_b * dir_b)))
    v = gathered_product(0, dir_a, dir_b, lambda: small_middle(0))
    block, scal = slab_values(0, v, small_end(0), lambda block, scal: (block, scal))
    norm, diag = scal[0:1], scal[1:2]

    def slab_inner(it, w):
        own = hx[it + 1, 1] * w[0:BAND].astype(F32) + hx[it + 1, 2] * w[BAND:].astype(F32)
        return rows_of(jnp.sum(own, 0, keepdims=True))

    w = filtered(1)
    image_a, image_b = scatter(1, w, lambda: small_start(1, slab_inner(0, w)), lambda: small_middle(1))
    step_len = norm / (diag + small_end(1)[0:1])
    image_a, image_b = image_a + kda[...] * dir_a, image_b + kdb[...] * dir_b
    sol_a, sol_b = step_len * dir_a, step_len * dir_b
    res_a, res_b = res_a - step_len * image_a, res_b - step_len * image_b
    scaled_a, scaled_b = pca[...] * res_a, pcb[...] * res_b
    small_start(
        2,
        rows_of(
            col_sum(res_a * scaled_a, res_b * scaled_b),
            col_sum(kda[...] * scaled_a * scaled_a, kdb[...] * scaled_b * scaled_b),
            col_sum(kda[...] * scaled_a * dir_a, kdb[...] * scaled_b * dir_b),
        ),
    )
    v = gathered_product(1, scaled_a, scaled_b, lambda: small_middle(2))

    def finish(new_block, scal):
        ratio = scal[0:1] / norm
        return new_block + ratio * block, scal

    _, scal = slab_values(1, v, small_end(2), finish)
    ratio = scal[0:1] / norm
    norm = scal[0:1]
    diag = scal[1:2] + 2.0 * ratio * scal[2:3] + ratio * ratio * diag
    dir_a, dir_b = scaled_a + ratio * dir_a, scaled_b + ratio * dir_b
    w = filtered(2)
    image_a, image_b = scatter(2, w, lambda: small_start(3, slab_inner(1, w)), lambda: small_middle(3))
    step_len = norm / (diag + small_end(3)[0:1])
    image_a, image_b = image_a + kda[...] * dir_a, image_b + kdb[...] * dir_b
    sol_a, sol_b = sol_a + step_len * dir_a, sol_b + step_len * dir_b
    res_a, res_b = res_a - step_len * image_a, res_b - step_len * image_b
    xout[0:NA] = sol_a[0:NA]
    xout[NA:] = sol_b[0:NB]
    rout[0:NA] = res_a[0:NA]
    rout[NA:] = res_b[0:NB]
    for copy in pending:
        copy.wait_send()


def toeplitz(pattern, band_len):
    tiled = jnp.tile(pattern, band_len)[: band_len * (2 * band_len - 1)]
    return tiled.reshape(band_len, 2 * band_len - 1)[:, :band_len]


def block_pair(filter_taps):
    band_len = filter_taps.shape[0]
    spacer = jnp.zeros((band_len,), jnp.float32)
    reversed_taps = filter_taps[:0:-1]
    lower = jnp.concatenate([filter_taps[:1], spacer, reversed_taps])
    upper = jnp.concatenate([jnp.zeros((1,), jnp.float32), reversed_taps, spacer])
    return (toeplitz(lower, band_len), toeplitz(upper, band_len))


def shards(design, observed, slab_counts, gap_mask, filter_taps, kaula_diag, precond):
    rows = observed.shape[0]
    own = NA + NB
    t = lax.axis_index(TM)
    pieces = design.reshape(rows, NZ, NY, own)
    piece_a = jnp.pad(pieces[..., :NA], ((0, 0), (0, 0), (0, 0), (0, RA - NA)))
    piece_b = jnp.pad(pieces[..., NA:], ((0, 0), (0, 0), (0, 0), (0, RB - NB)))
    aa = piece_a.transpose(1, 0, 2, 3).reshape(NZ, rows, NY * RA)
    ata = piece_a.transpose(1, 2, 3, 0).reshape(NZ, NY * RA, rows)
    ab = piece_b.transpose(2, 0, 1, 3).reshape(NY, rows, NZ * RB)
    atb = piece_b.transpose(2, 1, 3, 0).reshape(NY, NZ * RB, rows)
    position = jnp.arange(rows, dtype=jnp.int32)
    weight = ((gap_mask == 1) & (position < slab_counts[0])).astype(F32)
    wm = jnp.broadcast_to(weight[:, None], (rows, 128))
    lo, up = block_pair(filter_taps)

    def owned(diag):
        mine = lax.dynamic_slice_in_dim(diag, t * own, own, 0)
        part_a = jnp.pad(mine[:NA], (0, RA - NA))
        part_b = jnp.pad(mine[NA:], (0, RB - NB))
        return (
            jnp.broadcast_to(part_a[:, None], (RA, 128)),
            jnp.broadcast_to(part_b[:, None], (RB, 128)),
        )

    kda, kdb = owned(kaula_diag)
    pca, pcb = owned(precond)
    dma = pltpu.SemaphoreType.DMA
    args = (aa, ab, ata, atb, observed, wm, lo, up, lo.T, up.T, kda, kdb, pca, pcb)
    vm = pltpu.VMEM
    scratch = [
        vm((2 * BAND, 4 * BAND), F32),
        vm((NZ, NY, RA, 128), F32),
        vm((NZ, RB, 128), F32),
        vm((3, 2, 4, NY, RA, 128), F32),
        vm((3, 2, 4, NY, RA, 128), F32),
        vm((3, NY, RA, 128), F32),
        vm((3, NY, RA, 128), F32),
        vm((3, 2, 3, NZ // 2, RB, 128), F32),
        vm((3, 2, 3, NZ // 2, RB, 128), F32),
        vm((3, NZ, RB, 128), F32),
        vm((3, NZ, RB, 128), F32),
        vm((2, NZ, NY, RA, 128), BF16),
        vm((2, NY, NZ, RB, 128), BF16),
        vm((2, 2, BAND, 128), F32),
        vm((2, BAND, 128), F32),
        vm((2, BAND + 8, 128), F32),
        vm((2, NX, BAND + 8, 128), F32),
        vm((3, 4, BAND, 128), F32),
        vm((4, 2, 8, 128), F32),
        vm((4, NY + NZ, 8, 128), F32),
        vm((2, 2, 8, 128), F32),
        dma((3, 2, 4, NY)), dma((3, 2, 4, NY)), dma((3, NY)), dma((3, NY)),
        dma((3, 2, 3)), dma((3, 2, 3)), dma((3, NZ)), dma((3, NZ)),
        dma((2, 2, 2, 5, NZ)), dma((2, 2, 4, NY)), dma((2, NY)), dma((2, NZ)), dma((2, 2, 2, NZ)),
        dma((2, 2)), dma((2, 2)), dma((2, NX)), dma((2, NX)), dma((3, 6)), dma((3, 4)),
        dma((4, NY + NZ)), dma((4, NY + NZ)),
    ]
    out = jax.ShapeDtypeStruct((own, 128), F32)
    return pl.pallas_call(
        kernel,
        name="cg",
        out_shape=(out, out),
        in_specs=[pl.BlockSpec(memory_space=vm)] * len(args),
        out_specs=(pl.BlockSpec(memory_space=vm),) * 2,
        scratch_shapes=scratch,
        compiler_params=pltpu.CompilerParams(
            collective_id=0, has_side_effects=True, vmem_limit_bytes=60 * 1024 * 1024
        ),
    )(*args)


def solution(mesh):
    torus = Mesh(mesh.devices.reshape(NZ, NY, NX, NC), AXES)
    in_specs = (P(TM, COEF), P(TM, None), P(TM), P(TM), P(), P(COEF), P(COEF))
    out_specs = (P((*COEF, *TM), None),) * 2
    return jax.shard_map(shards, mesh=torus, in_specs=in_specs, out_specs=out_specs, check_vma=False)
```

time: 598 us -> 231 us (0.39)
  blocking collectives: 276 us -> 0 us
  Pallas kernels: 0 us -> 195 us
  waiting for transfers between devices: 166 us -> 0 us
  starting transfers between devices: 44.4 us -> 0 us
  local copies, waits for them, and re-layouts: 62.9 us -> 29.3 us
  matrix products: 26.6 us -> 0 us
  other arithmetic: 17.7 us -> 3.87 us
    pallas_call x0 -> x1, Pallas kernels: none -> 195 us  [shards(): pl.pallas_call(kernel, name='cg', out_shape=(out, out), in_specs=[pl.Bloc...]
    all_to_all x4 -> x0, blocking collectives: 193 us -> none  [the longest x3 110 us: from_everyone(): return lax.all_to_all(copies, axis, split_axis=0, concat_axis=0, tiled=True)]
    all_to_all x3 -> x0, waiting for transfers between devices: 157 us -> none  [the longest x2 142 us: summed_on_arrival(): tiles = lax.all_to_all(split_up(array, dim, count), axis, 0, 0, tiled=True)]
    psum x8 -> x0, blocking collectives: 83.5 us -> none  [one_axis_at_a_time(): return functools.reduce(lax.psum, axes, array)]
    all_to_all x3 -> x0, starting transfers between devices: 30.2 us -> none  [the longest x2 20.9 us: summed_on_arrival(): tiles = lax.all_to_all(split_up(array, dim, count), axis, 0, 0, tiled=True)]
    dot_general x17 -> x0, matrix products: 26.6 us -> none  [the longest x3 8.64 us: transposed_term(): lax.dot_general(design, filtered, (((0,), (0,)), ((), ())), preferred_ele...]
    dot_general x5 -> x0, local copies, waits for them, and re-layouts: 18 us -> none  [the longest x3 14.6 us: transposed_term(): lax.dot_general(design, filtered, (((0,), (0,)), ((), ())), preferred_ele...]
    reshape x8 -> x3, local copies, waits for them, and re-layouts: 23.4 us -> 8.02 us  [the longest x1 3.68 us: shards(): pieces = design.reshape(rows, NZ, NY, own)]
  transfers between devices with their start and end apart: 9 -> 0, of which waited for: 7 -> 0; matrix products, arithmetic and copies ran while one was open for 3% -> 0% of each run, Pallas kernels for 0% -> 0%
where the time goes in v1:
time: 231 us; the launch traced here: 230 us
  Pallas kernels  195 us (84%)
  local copies, waits for them, and re-layouts  29.3 us (13%)
  other arithmetic  3.87 us (2%)
    pallas_call x1, Pallas kernels, shards(): pl.pallas_call(kernel, name='cg', out_shape=(out, out), in_specs=[pl.Bloc...  195 us
    unnamed x18, local copies, waits for them, and re-layouts  12.7 us

profile of v1, /device:TPU:1, one launch (start us, length us, event | category | flops | bytes accessed | tf_op | source)
XLA Modules:
  0.0 230.0 jit_solution(10288971329991124129)
XLA Ops:
  1.3 0.7 and_convert_fusion
  2.0 0.7 slice.42
  2.7 0.1 rev.3
  2.8 0.8 dynamic_slice.6
  3.6 0.8 dynamic_slice.7
  4.3 0.1 slice.50
  4.4 0.7 slice_select_fusion.1
  5.1 0.1 slice.48
  5.2 0.7 pad_maximum_fusion.1
  5.9 0.7 broadcast_in_dim.15.kdb
  6.6 0.7 broadcast_in_dim.17.pcb
  7.3 0.7 broadcast_in_dim.16.pca
  8.0 0.7 broadcast_in_dim.14.kda
  8.6 0.7 broadcast_in_dim.12.wm
  9.4 0.1 copy.27
  9.5 0.3 reshape.38
  9.8 0.0 copy-start.2
  9.8 0.7 copy.25
  10.6 0.1 copy.26
  10.6 0.3 reshape.37
  11.0 0.0 copy-start.3
  11.0 0.7 copy.24
  11.7 5.6 %copy.15 = bf16[256,6272]{0,1:T(8,128)(2,1)} copy(bf16[256,6272]{1,0:T(8,128)(2,1)} %param.7) | data formatting | bytes 6422528 | tf_op args[0]
  17.3 0.0 copy-done.2
  17.3 0.0 copy-done.3
  17.3 3.7 %reshape.32 = bf16[256,8,4,196]{0,3,2,1:T(8,128)(2,1)S(1)} reshape(bf16[256,6272]{0,1:T(8,128)(2,1)} %copy.15) | data formatting | bytes 6422528 | tf_op jit(solution)/shard_map/reshape | solution.py:387
  21.0 0.0 copy-start.1
  21.0 1.7 copy-done.1
  22.7 0.0 copy-start.4
  22.7 0.7 copy-done.4
  23.4 0.0 slice-start
  23.4 1.8 slice_select_fusion
  25.2 0.0 copy-start
  25.2 0.1 slice-done
  25.3 0.4 pad_bitcast_fusion
  25.7 1.3 copy.17
  27.0 0.1 copy.16
  27.1 1.6 copy.21.ab
  28.7 0.0 copy-done
  28.7 2.7 %copy.20.aa = bf16[8,256,448]{2,1,0:T(8,128)(2,1)} copy(bf16[8,256,448]{1,2,0:T(8,128)(2,1)S(1)} %bitcast.27) | data formatting | bytes 3670016 | tf_op jit(solution)/shard_map/reshape | solution.py:390
  31.4 195.4 %cg.1 = (f32[196,128]{1,0:T(8,128)}, f32[196,128]{1,0:T(8,128)}) custom-call(bf16[8,256,448]{2,1,0:T(8,128)(2,1)} %copy.20.aa, bf16[4,256,768]{2,1,0:T(8,128)(2,1)} %copy.21.ab, bf16[8,448,256]{2,1,0:T(8,128)(2,1)} %bitcast.28, bf16[4,768,256]{2,1,0:T(8,128)(2,1)} %bitcast.30, f32[256,128]{1,0:T(8,128)} %obs.1, f32[256,128]{1,0:T(8,128)} %broadcast_in_dim.12.wm, ...), custom_call_target="tpu_custom_call" | custom-call | tf_op jit(solution)/shard_map/cg/pallas_call | solution.py:442
  226.9 1.5 copy.31
  228.4 1.5 copy.32
  (6 shorter events, 0.0 us)
Async XLA Ops:
  9.8 7.5 %copy-start.2 = (f32[128,128]{1,0:T(8,128)}, f32[128,128]{1,0:T(8,128)S(1)}, u32[]{:S(2)}) copy-start(f32[128,128]{1,0:T(8,128)S(1)} %slice.56.up) | copy-start | bytes 196612
  11.0 6.3 %copy-start.3 = (f32[128,128]{1,0:T(8,128)}, f32[128,128]{1,0:T(8,128)S(1)}, u32[]{:S(2)}) copy-start(f32[128,128]{1,0:T(8,128)S(1)} %slice.54.lo) | copy-start | bytes 196612
  21.0 1.7 copy-start.1
  22.7 0.7 copy-start.4
  23.4 2.0 slice-start
  25.2 3.5 %copy-start = (bf16[256,8,4,112]{0,3,2,1:T(8,128)(2,1)}, bf16[256,8,4,112]{0,3,2,1:T(8,128)(2,1)S(1)}, u32[]{:S(2)}) copy-start(bf16[256,8,4,112]{0,3,2,1:T(8,128)(2,1)S(1)} %slice_select_fusion) | copy-start | bytes 5505028

commit v2 on v1

--- a/solution.py
+++ b/solution.py
@@ -13,8 +13,13 @@
 COEF = ("x", "c")
 MESH = pl.DeviceIdType.MESH
 NZ, NY, NX, NC = 8, 4, 4, 2
-NA, NB = 104, 92
-RA, RB = 112, 96
+NA, NB = 92, 104
+RA, RB = 96, 112
+OWN = NA + NB
+LANES = 128
+WIDE = 3 * LANES
+I16 = jnp.int16
+I32 = jnp.int32
 BAND = 128
 F32 = jnp.float32
 BF16 = jnp.bfloat16
@@ -25,6 +30,39 @@
     return jnp.dot(a, b, preferred_element_type=F32, precision=precision)
 
 
+def dot_t(a, b, precision=None):
+    return lax.dot_general(a, b, (((1,), (1,)), ((), ())), preferred_element_type=F32, precision=precision)
+
+
+def encoded(v, spare):
+    top = jnp.maximum(jnp.max(jnp.abs(v), axis=-2, keepdims=True), 1e-30)
+    power = jnp.floor(jnp.log2(top)) + 1.0
+    q = jnp.clip(jnp.round(v * jnp.exp2(15.0 - power)), -32767.0, 32767.0)
+    row = lax.broadcasted_iota(I32, v.shape, v.ndim - 2)
+    return jnp.where(row == spare, power, q).astype(I32).astype(I16)
+
+
+def decoded(q, spare):
+    v = q.astype(I32).astype(F32)
+    return v * jnp.exp2(v[..., spare : spare + 1, :] - 15.0)
+
+
+def enc_a(v):
+    return encoded(v, NA)
+
+
+def enc_b(v):
+    return encoded(v, NB)
+
+
+def dec_a(q):
+    return decoded(q, NA)
+
+
+def dec_b(q):
+    return decoded(q, NB)
+
+
 def rcopy(src, dst, ssem, rsem, **device):
     return pltpu.make_async_remote_copy(
         src_ref=src, dst_ref=dst, send_sem=ssem, recv_sem=rsem, device_id=device, device_id_type=MESH
@@ -32,9 +70,9 @@
 
 
 def kernel(
-    aa, ab, ata, atb, obs, wm, lo, up, lot, upt, kda, kdb, pca, pcb,
+    design, obs, counts, gaps, taps, kaula, precond,
     xout, rout,
-    bm, y_a, y_b,
+    aa, ab, ata, atb, wm, kda, kdb, pca, pcb, column, bm, y_a, y_b, y_c,
     sa, ra, sya, rya, sb, rb, szb, rzb,
     ga, gb, vs, vr, us, ur, hx, scs, scr, scc,
     sem_sa, sem_ra, sem_sya, sem_rya, sem_sb, sem_rb, sem_szb, sem_rzb,
@@ -72,10 +110,15 @@
 
     keep_first = jnp.where(t == 0, 0.0, 1.0).astype(F32)
     keep_last = jnp.where(t == NZ * NY - 1, 0.0, 1.0).astype(F32)
-    ll = dot(lot[...], lo[...], HIGH)
-    uu = dot(upt[...], up[...], HIGH)
-    lu = dot(lot[...], up[...], HIGH)
-    ul = dot(upt[...], lo[...], HIGH)
+    row = lax.broadcasted_iota(I32, (BAND, BAND), 0)
+    col = lax.broadcasted_iota(I32, (BAND, BAND), 1)
+    rolled = pltpu.roll(jnp.broadcast_to(taps[...], (BAND, BAND)), 0, 1, stride=1, stride_axis=0)
+    lot = jnp.where(col >= row, rolled, 0.0)
+    upt = jnp.where(col < row, rolled, 0.0)
+    ll = dot_t(lot, lot, HIGH)
+    uu = dot_t(upt, upt, HIGH)
+    lu = dot_t(lot, upt, HIGH)
+    ul = dot_t(upt, lot, HIGH)
     zero = jnp.zeros((BAND, BAND), F32)
     bm[0:BAND, 0:BAND] = keep_first * lu
     bm[0:BAND, BAND : 2 * BAND] = ll + uu
@@ -86,6 +129,57 @@
     bm[BAND:, 2 * BAND : 3 * BAND] = ll + keep_last * uu
     bm[BAND:, 3 * BAND :] = keep_last * ul
 
+    for b in range(2):
+        on = (gaps[b : b + 1, :] == 1) & (col[0:1] + b * BAND < counts[0])
+        wm[b * BAND : (b + 1) * BAND] = jnp.broadcast_to(jnp.where(on, 1.0, 0.0), (BAND, BAND)).T
+
+    line = lax.div(t * OWN, LANES)
+    shift = t * OWN - line * LANES
+    for diag, part_a, part_b in ((kaula, kda, kdb), (precond, pca, pcb)):
+        for k in range(3):
+            values = diag[pl.ds(jnp.minimum(line + k, diag.shape[0] - 1), 1), :]
+            column[k * LANES : (k + 1) * LANES] = jnp.broadcast_to(values, (LANES, LANES)).T
+        row_a = lax.broadcasted_iota(I32, (RA, LANES), 0)
+        row_b = lax.broadcasted_iota(I32, (RB, LANES), 0)
+        part_a[...] = jnp.where(row_a < NA, column[pl.ds(shift, RA), :], 0.0)
+        part_b[...] = jnp.where(row_b < NB, column[pl.ds(shift + NA, RB), :], 0.0)
+
+    def picked(p):
+        first = jnp.minimum(lax.div(p * OWN, LANES), design.shape[1] // LANES - 3)
+        window = design[:, pl.ds(pl.multiple_of(first * LANES, LANES), WIDE)]
+        place = lax.broadcasted_iota(I32, (2 * LANES, WIDE), 0)
+        wanted = jnp.where(place < LANES, place, place - LANES + NA)
+        real = ((place < NA) | (place >= LANES)) & (place < LANES + NB)
+        at = lax.broadcasted_iota(I32, (2 * LANES, WIDE), 1) - (p * OWN - first * LANES)
+        return window, jnp.where((at == wanted) & real, 1.0, 0.0).astype(BF16)
+
+    def put_rows(p, carry):
+        window, pick = picked(p)
+        rows = dot_t(pick, window).astype(BF16)
+        zz, yy = lax.div(p, NY), lax.rem(p, NY)
+        ata[zz, yy] = rows[0:RA]
+        atb[yy, zz] = rows[LANES : LANES + RB]
+        return carry
+
+    def put_columns(p, carry):
+        window, pick = picked(p)
+        columns = dot_t(window, pick).astype(BF16)
+        zz, yy = lax.div(p, NY), lax.rem(p, NY)
+        aa[zz, :, pl.ds(pl.multiple_of(yy * LANES, LANES), LANES)] = columns[:, 0:LANES]
+        ab[yy, :, pl.ds(pl.multiple_of(zz * LANES, LANES), LANES)] = columns[:, LANES:]
+        for it in range(2):
+            ga[it, zz, yy, RA:] = jnp.zeros((LANES - RA, LANES), BF16)
+            gb[it, yy, zz, RB:] = jnp.zeros((LANES - RB, LANES), BF16)
+        return carry
+
+    lax.fori_loop(0, NZ * NY, put_rows, 0)
+
+    def at_a(target):
+        return ata[target].reshape(NY * RA, 2 * BAND)
+
+    def at_b(target):
+        return atb[target].reshape(NZ * RB, 2 * BAND)
+
     def filtered(st):
         ext = hx[st].reshape(4 * BAND, BAND)
         return (wm[...] * dot(bm[...], ext, HIGH)).astype(BF16)
@@ -114,30 +208,30 @@
     half = NZ // 2 * RB
 
     def scatter(st, w, early, late):
-        part = dot(atb[yp[2]], w).reshape(2, NZ // 2, RB, 128)
+        part = dot(at_b(yp[2]), w).reshape(2, NZ // 2, RB, 128)
         for way, peer in ((0, yp[1]), (1, ym[1])):
-            sb[st, way, 0] = part[way]
+            sb[st, way, 0] = enc_b(part[way])
             send(sb.at[st, way, 0], rb.at[st, way, 0], sem_sb.at[st, way, 0], sem_rb.at[st, way, 0], y=peer)
         for way, target, peer in ((0, zp[4], zp[1]), (1, zm[3], zm[1])):
-            sa[st, way, 0] = dot(ata[target], w).reshape(NY, RA, 128)
+            sa[st, way, 0] = enc_a(dot(at_a(target), w).reshape(NY, RA, 128))
             for j in range(NY):
                 send(
                     sa.at[st, way, 0, j], ra.at[st, way, 0, j],
                     sem_sa.at[st, way, 0, j], sem_ra.at[st, way, 0, j], z=peer,
                 )
         for way, peer in ((0, yp[1]), (1, ym[1])):
-            part = dot(atb[peer], w).reshape(2, NZ // 2, RB, 128)
-            sb[st, way, 1] = part[1 - way]
+            part = dot(at_b(peer), w).reshape(2, NZ // 2, RB, 128)
+            sb[st, way, 1] = enc_b(part[1 - way])
             send(sb.at[st, way, 1], rb.at[st, way, 1], sem_sb.at[st, way, 1], sem_rb.at[st, way, 1], y=peer)
-            sb[st, way, 2] = part[way]
+            y_c[way] = part[way]
 
         def product(i, carry):
-            target = lax.rem(z + 5 + jnp.where(i < 3, 0, 0) + i, NZ)
-            y_a[target] = dot(ata[target], w).reshape(NY, RA, 128)
+            target = lax.rem(z + 5 + i, NZ)
+            y_a[target] = dot(at_a(target), w).reshape(NY, RA, 128)
             return carry
 
         lax.fori_loop(1, NZ - 1, product, 0)
-        y_b[...] = dot(atb[y], w).reshape(NZ, RB, 128)
+        y_b[...] = dot(at_b(y), w).reshape(NZ, RB, 128)
         early()
         for s in range(1, 4):
             for j in range(NY):
@@ -147,7 +241,7 @@
                     arrived(
                         ra.at[st, way, s - 1, j], sem_sa.at[st, way, s - 1, j], sem_ra.at[st, way, s - 1, j], z=peer
                     )
-                    sa[st, way, s, j] = ra[st, way, s - 1, j] + y_a[target, j]
+                    sa[st, way, s, j] = enc_a(dec_a(ra[st, way, s - 1, j]) + y_a[target, j])
                     send(
                         sa.at[st, way, s, j], ra.at[st, way, s, j],
                         sem_sa.at[st, way, s, j], sem_ra.at[st, way, s, j], z=peer,
@@ -155,7 +249,7 @@
             if s == 1:
                 for way, peer in ((0, yp[1]), (1, ym[1])):
                     arrived(rb.at[st, way, 0], sem_sb.at[st, way, 0], sem_rb.at[st, way, 0], y=peer)
-                    sb[st, way, 2] = sb[st, way, 2] + rb[st, way, 0]
+                    sb[st, way, 2] = enc_b(y_c[way] + dec_b(rb[st, way, 0]))
                     send(
                         sb.at[st, way, 2], rb.at[st, way, 2], sem_sb.at[st, way, 2], sem_rb.at[st, way, 2], y=peer
                     )
@@ -166,63 +260,75 @@
                         arrived(
                             rb.at[st, way, kind], sem_sb.at[st, way, kind], sem_rb.at[st, way, kind], y=peer
                         )
-                szb[st, 0 : NZ // 2] = y_b[0 : NZ // 2] + rb[st, 0, 2] + rb[st, 1, 1]
-                szb[st, NZ // 2 :] = y_b[NZ // 2 :] + rb[st, 0, 1] + rb[st, 1, 2]
+                low = y_b[0 : NZ // 2] + dec_b(rb[st, 0, 2]) + dec_b(rb[st, 1, 1])
+                y_b[0 : NZ // 2] = low
+                szb[st, 0 : NZ // 2] = enc_b(low)
+                high = y_b[NZ // 2 :] + dec_b(rb[st, 0, 1]) + dec_b(rb[st, 1, 2])
+                y_b[NZ // 2 :] = high
+                szb[st, NZ // 2 :] = enc_b(high)
                 for k in (4, 3, 5, 2, 6, 1, 7):
                     send(szb.at[st, zp[k]], rzb.at[st, k], sem_szb.at[st, k], sem_rzb.at[st, k], z=zp[k])
         for j in range(NY):
             arrived(ra.at[st, 0, 3, j], sem_sa.at[st, 0, 3, j], sem_ra.at[st, 0, 3, j], z=zp[1])
             arrived(ra.at[st, 1, 2, j], sem_sa.at[st, 1, 2, j], sem_ra.at[st, 1, 2, j], z=zm[1])
-            sya[st, j] = ra[st, 0, 3, j] + ra[st, 1, 2, j] + y_a[z, j]
+            total = dec_a(ra[st, 0, 3, j]) + dec_a(ra[st, 1, 2, j]) + y_a[z, j]
+            y_a[z, j] = total
+            sya[st, j] = enc_a(total)
         for k in (2, 1, 3):
             send(sya.at[st, yp[k]], rya.at[st, k], sem_sya.at[st, k], sem_rya.at[st, k], y=yp[k])
-        sum_b = szb[st, z]
+        sum_b = y_b[z]
         for k in range(1, NZ):
             arrived(rzb.at[st, k], sem_szb.at[st, k], sem_rzb.at[st, k], z=zp[k])
-            sum_b = sum_b + rzb[st, k]
-        sum_a = sya[st, y]
+            sum_b = sum_b + dec_b(rzb[st, k])
+        sum_a = y_a[z, y]
         for k in range(1, NY):
             arrived(rya.at[st, k], sem_sya.at[st, k], sem_rya.at[st, k], y=yp[k])
-            sum_a = sum_a + rya[st, k]
+            sum_a = sum_a + dec_a(rya[st, k])
         return sum_a, sum_b
 
     first_half, second_half = (0, 1, 7, 2), (6, 3, 5, 4)
 
     def gathered_product(it, rows_a, rows_b, middle):
-        ga[it, z, y] = rows_a.astype(BF16)
-        gb[it, y, z] = rows_b.astype(BF16)
+        ga[it, z, y, 0:RA] = rows_a.astype(BF16)
+        gb[it, y, z, 0:RB] = rows_b.astype(BF16)
+
+        def part_a(it, zz, yy):
+            return ga.at[it, zz, yy, pl.ds(0, RA)]
+
+        def part_b(it, yy, zz):
+            return gb.at[it, yy, zz, pl.ds(0, RB)]
 
         def put_a(way, s, k):
             zz, yy = (zm[s] if way == 0 else zp[s]), ym[k]
             peer = zp[1] if way == 0 else zm[1]
-            send(ga.at[it, zz, yy], ga.at[it, zz, yy], sem_gs.at[it, 0, way, s, k], sem_ga.at[it, way, s, k], z=peer)
+            send(part_a(it, zz, yy), part_a(it, zz, yy), sem_gs.at[it, 0, way, s, k], sem_ga.at[it, way, s, k], z=peer)
 
         def got_a(way, s, k):
             zz, yy = (zm[s + 1] if way == 0 else zp[s + 1]), ym[k]
-            arrived(ga.at[it, zz, yy], sem_gs.at[it, 0, way, s, k], sem_ga.at[it, way, s, k], z=zp[1])
+            arrived(part_a(it, zz, yy), sem_gs.at[it, 0, way, s, k], sem_ga.at[it, way, s, k], z=zp[1])
 
         def put_b(way, s, k):
             zz, yy = zm[k], (ym[s] if way == 0 else yp[s])
             peer = yp[1] if way == 0 else ym[1]
-            send(gb.at[it, yy, zz], gb.at[it, yy, zz], sem_gs.at[it, 1, way, s, k], sem_gby.at[it, way, s, k], y=peer)
+            send(part_b(it, yy, zz), part_b(it, yy, zz), sem_gs.at[it, 1, way, s, k], sem_gby.at[it, way, s, k], y=peer)
 
         def got_b(way, s, k):
             zz, yy = zm[k], (ym[s + 1] if way == 0 else yp[s + 1])
-            arrived(gb.at[it, yy, zz], sem_gs.at[it, 1, way, s, k], sem_gby.at[it, way, s, k], y=yp[1])
+            arrived(part_b(it, yy, zz), sem_gs.at[it, 1, way, s, k], sem_gby.at[it, way, s, k], y=yp[1])
 
         for k in (2, 1, 3):
-            send(ga.at[it, z, y], ga.at[it, z, y], sem_gs.at[it, 0, 0, 4, k], sem_gay.at[it, k], y=yp[k])
+            send(part_a(it, z, y), part_a(it, z, y), sem_gs.at[it, 0, 0, 4, k], sem_gay.at[it, k], y=yp[k])
         put_a(0, 0, 0)
         put_a(1, 0, 0)
         for k in (4, 3, 5, 2, 6, 1, 7):
-            send(gb.at[it, y, z], gb.at[it, y, z], sem_gs.at[it, 1, 0, 2, k], sem_gb.at[it, k], z=zp[k])
+            send(part_b(it, y, z), part_b(it, y, z), sem_gs.at[it, 1, 0, 2, k], sem_gb.at[it, k], z=zp[k])
         put_b(0, 0, 0)
         put_b(1, 0, 0)
         for k in (1, 3, 2):
-            arrived(ga.at[it, z, ym[k]], sem_gs.at[it, 0, 0, 4, k], sem_gay.at[it, k], y=yp[k])
+            arrived(part_a(it, z, ym[k]), sem_gs.at[it, 0, 0, 4, k], sem_gay.at[it, k], y=yp[k])
             put_a(0, 0, k)
             put_a(1, 0, k)
-        v = dot(aa[z], ga[it, z].reshape(NY * RA, 128))
+        v = dot(aa[z], ga[it, z].reshape(NY * LANES, LANES))
         for s in range(1, 4):
             for k in (0, 1, 3, 2):
                 got_a(0, s - 1, k)
@@ -232,7 +338,7 @@
                     put_a(1, s, k)
             if s == 1:
                 for k in (1, 7, 2, 6, 3, 5, 4):
-                    arrived(gb.at[it, y, zm[k]], sem_gs.at[it, 1, 0, 2, k], sem_gb.at[it, k], z=zp[k])
+                    arrived(part_b(it, y, zm[k]), sem_gs.at[it, 1, 0, 2, k], sem_gb.at[it, k], z=zp[k])
                     put_b(0, 0, k)
                     put_b(1, 0, k)
             if s == 2:
@@ -243,23 +349,23 @@
                     got_b(1, 0, k)
                     put_b(1, 1, k)
                 middle()
-            v = v + dot(aa[zm[s]], ga[it, zm[s]].reshape(NY * RA, 128))
-            v = v + dot(aa[zp[s]], ga[it, zp[s]].reshape(NY * RA, 128))
-        v = v + dot(ab[y], gb[it, y].reshape(NZ * RB, 128))
+            v = v + dot(aa[zm[s]], ga[it, zm[s]].reshape(NY * LANES, LANES))
+            v = v + dot(aa[zp[s]], ga[it, zp[s]].reshape(NY * LANES, LANES))
+        v = v + dot(ab[y], gb[it, y].reshape(NZ * LANES, LANES))
         for k in second_half:
             got_b(0, 0, k)
         for k in first_half:
             got_b(1, 0, k)
-        v = v + dot(ab[yp[1]], gb[it, yp[1]].reshape(NZ * RB, 128))
-        v = v + dot(ab[ym[1]], gb[it, ym[1]].reshape(NZ * RB, 128))
+        v = v + dot(ab[yp[1]], gb[it, yp[1]].reshape(NZ * LANES, LANES))
+        v = v + dot(ab[ym[1]], gb[it, ym[1]].reshape(NZ * LANES, LANES))
         for k in first_half:
             got_b(0, 1, k)
         for k in second_half:
             got_b(1, 1, k)
-        v = v + dot(ab[yp[2]], gb[it, yp[2]].reshape(NZ * RB, 128))
+        v = v + dot(ab[yp[2]], gb[it, yp[2]].reshape(NZ * LANES, LANES))
         for k in range(NY):
             got_a(0, 3, k)
-        return v + dot(aa[zm[4]], ga[it, zm[4]].reshape(NY * RA, 128))
+        return v + dot(aa[zm[4]], ga[it, zm[4]].reshape(NY * LANES, LANES))
 
     def slab_values(it, v, scal, finish):
         vs[it] = v.reshape(2, BAND, 128)
@@ -307,7 +413,7 @@
     arrived(hx.at[0, 0], sem_hs.at[0, 0], sem_hr.at[0, 0], c=other)
     arrived(hx.at[0, 3], sem_hs.at[0, 3], sem_hr.at[0, 3], c=other)
     nothing = lambda: None
-    res_a, res_b = scatter(0, filtered(0), nothing, nothing)
+    res_a, res_b = scatter(0, filtered(0), lambda: lax.fori_loop(0, NZ * NY, put_columns, 0), nothing)
 
     def col_sum(a, b):
         return jnp.sum(a, 0, keepdims=True) + jnp.sum(b, 0, keepdims=True)
@@ -366,64 +472,37 @@
         copy.wait_send()
 
 
-def toeplitz(pattern, band_len):
-    tiled = jnp.tile(pattern, band_len)[: band_len * (2 * band_len - 1)]
-    return tiled.reshape(band_len, 2 * band_len - 1)[:, :band_len]
-
-
-def block_pair(filter_taps):
-    band_len = filter_taps.shape[0]
-    spacer = jnp.zeros((band_len,), jnp.float32)
-    reversed_taps = filter_taps[:0:-1]
-    lower = jnp.concatenate([filter_taps[:1], spacer, reversed_taps])
-    upper = jnp.concatenate([jnp.zeros((1,), jnp.float32), reversed_taps, spacer])
-    return (toeplitz(lower, band_len), toeplitz(upper, band_len))
-
-
 def shards(design, observed, slab_counts, gap_mask, filter_taps, kaula_diag, precond):
     rows = observed.shape[0]
-    own = NA + NB
-    t = lax.axis_index(TM)
-    pieces = design.reshape(rows, NZ, NY, own)
-    piece_a = jnp.pad(pieces[..., :NA], ((0, 0), (0, 0), (0, 0), (0, RA - NA)))
-    piece_b = jnp.pad(pieces[..., NA:], ((0, 0), (0, 0), (0, 0), (0, RB - NB)))
-    aa = piece_a.transpose(1, 0, 2, 3).reshape(NZ, rows, NY * RA)
-    ata = piece_a.transpose(1, 2, 3, 0).reshape(NZ, NY * RA, rows)
-    ab = piece_b.transpose(2, 0, 1, 3).reshape(NY, rows, NZ * RB)
-    atb = piece_b.transpose(2, 1, 3, 0).reshape(NY, NZ * RB, rows)
-    position = jnp.arange(rows, dtype=jnp.int32)
-    weight = ((gap_mask == 1) & (position < slab_counts[0])).astype(F32)
-    wm = jnp.broadcast_to(weight[:, None], (rows, 128))
-    lo, up = block_pair(filter_taps)
-
-    def owned(diag):
-        mine = lax.dynamic_slice_in_dim(diag, t * own, own, 0)
-        part_a = jnp.pad(mine[:NA], (0, RA - NA))
-        part_b = jnp.pad(mine[NA:], (0, RB - NB))
-        return (
-            jnp.broadcast_to(part_a[:, None], (RA, 128)),
-            jnp.broadcast_to(part_b[:, None], (RB, 128)),
-        )
-
-    kda, kdb = owned(kaula_diag)
-    pca, pcb = owned(precond)
+    coefs = design.shape[1]
     dma = pltpu.SemaphoreType.DMA
-    args = (aa, ab, ata, atb, observed, wm, lo, up, lo.T, up.T, kda, kdb, pca, pcb)
+    args = (
+        design, observed, slab_counts, gap_mask.reshape(rows // LANES, LANES), filter_taps.reshape(1, LANES),
+        kaula_diag.reshape(coefs // LANES, LANES), precond.reshape(coefs // LANES, LANES),
+    )
     vm = pltpu.VMEM
     scratch = [
+        vm((NZ, rows, NY * LANES), BF16),
+        vm((NY, rows, NZ * LANES), BF16),
+        vm((NZ, NY, RA, rows), BF16),
+        vm((NY, NZ, RB, rows), BF16),
+        vm((rows, LANES), F32),
+        vm((RA, LANES), F32), vm((RB, LANES), F32), vm((RA, LANES), F32), vm((RB, LANES), F32),
+        vm((4 * LANES, LANES), F32),
         vm((2 * BAND, 4 * BAND), F32),
         vm((NZ, NY, RA, 128), F32),
         vm((NZ, RB, 128), F32),
-        vm((3, 2, 4, NY, RA, 128), F32),
-        vm((3, 2, 4, NY, RA, 128), F32),
-        vm((3, NY, RA, 128), F32),
-        vm((3, NY, RA, 128), F32),
-        vm((3, 2, 3, NZ // 2, RB, 128), F32),
-        vm((3, 2, 3, NZ // 2, RB, 128), F32),
-        vm((3, NZ, RB, 128), F32),
-        vm((3, NZ, RB, 128), F32),
-        vm((2, NZ, NY, RA, 128), BF16),
-        vm((2, NY, NZ, RB, 128), BF16),
+        vm((2, NZ // 2, RB, 128), F32),
+        vm((3, 2, 4, NY, RA, 128), I16),
+        vm((3, 2, 4, NY, RA, 128), I16),
+        vm((3, NY, RA, 128), I16),
+        vm((3, NY, RA, 128), I16),
+        vm((3, 2, 3, NZ // 2, RB, 128), I16),
+        vm((3, 2, 3, NZ // 2, RB, 128), I16),
+        vm((3, NZ, RB, 128), I16),
+        vm((3, NZ, RB, 128), I16),
+        vm((2, NZ, NY, LANES, LANES), BF16),
+        vm((2, NY, NZ, LANES, LANES), BF16),
         vm((2, 2, BAND, 128), F32),
         vm((2, BAND, 128), F32),
         vm((2, BAND + 8, 128), F32),
@@ -438,12 +517,12 @@
         dma((2, 2)), dma((2, 2)), dma((2, NX)), dma((2, NX)), dma((3, 6)), dma((3, 4)),
         dma((4, NY + NZ)), dma((4, NY + NZ)),
     ]
-    out = jax.ShapeDtypeStruct((own, 128), F32)
+    out = jax.ShapeDtypeStruct((OWN, LANES), F32)
     return pl.pallas_call(
         kernel,
         name="cg",
         out_shape=(out, out),
-        in_specs=[pl.BlockSpec(memory_space=vm)] * len(args),
+        in_specs=[pl.BlockSpec(memory_space=pltpu.SMEM if i == 2 else vm) for i in range(len(args))],
         out_specs=(pl.BlockSpec(memory_space=vm),) * 2,
         scratch_shapes=scratch,
         compiler_params=pltpu.CompilerParams(

time: 231 us -> 174 us (0.75)
  local copies, waits for them, and re-layouts: 29.3 us -> 3.09 us
  Pallas kernels: 195 us -> 169 us
  other arithmetic: 3.87 us -> 0 us
    pallas_call x1, Pallas kernels: 195 us -> 169 us  [shards(): pl.pallas_call(kernel, name='cg', out_shape=(out, out), in_specs=[pl.Bloc...]
    unnamed x18 -> x2, local copies, waits for them, and re-layouts: 12.7 us -> 3.09 us
    reshape x5 -> x0, local copies, waits for them, and re-layouts: 8.69 us -> none  [the longest x1 3.68 us: shards(): pieces = design.reshape(rows, NZ, NY, own)]
    broadcast_in_dim x6 -> x0, local copies, waits for them, and re-layouts: 3.51 us -> none  [the longest x2 1.39 us: owned(): jnp.broadcast_to(part_b[:, None], (RB, 128))]
    pad x2 -> x0, other arithmetic: 2.47 us -> none  [the longest x1 1.81 us: shards(): piece_a = jnp.pad(pieces[..., :NA], ((0, 0), (0, 0), (0, 0), (0, RA - NA)))]
where the time goes in v2:
time: 174 us
  Pallas kernels  169 us (97%)
  local copies, waits for them, and re-layouts  3.09 us (2%)
    pallas_call x1, Pallas kernels, shards(): pl.pallas_call(kernel, name='cg', out_shape=(out, out), in_specs=[pl.Bloc...  169 us

profile of v2, /device:TPU:1, one launch (start us, length us, event | category | flops | bytes accessed | tf_op | source)
XLA Modules:
  0.0 173.8 jit_solution(670752791467943799)
XLA Ops:
  1.3 169.4 %cg.1 = (f32[196,128]{1,0:T(8,128)}, f32[196,128]{1,0:T(8,128)}) custom-call(bf16[256,6272]{1,0:T(8,128)(2,1)} %design.1, f32[256,128]{1,0:T(8,128)} %obs.1, s32[1]{0:T(128)S(6)} %copy.11.counts, s32[2,128]{1,0:T(2,128)} %bitcast.6, f32[1,128]{1,0:T(1,128)} %bitcast.7, f32[49,128]{1,0:T(8,128)} %bitcast.4, f32[49,128]{1,0:T(8,128)} %bitcast.5), custom_call_target="tpu_custom_call" | custom-call | tf_op jit(solution)/shard_map/cg/pallas_call | solution.py:521
  170.7 1.5 copy.12
  172.2 1.5 copy.13

commit v3 on v2

--- a/solution.py
+++ b/solution.py
@@ -63,6 +63,14 @@
     return decoded(q, NB)
 
 
+def enc_v(v):
+    return encoded(jnp.concatenate([v, jnp.zeros((16, LANES), F32)], 0), BAND)
+
+
+def dec_v(q):
+    return decoded(q, BAND)[..., 0:BAND, :]
+
+
 def rcopy(src, dst, ssem, rsem, **device):
     return pltpu.make_async_remote_copy(
         src_ref=src, dst_ref=dst, send_sem=ssem, recv_sem=rsem, device_id=device, device_id_type=MESH
@@ -74,10 +82,10 @@
     xout, rout,
     aa, ab, ata, atb, wm, kda, kdb, pca, pcb, column, bm, y_a, y_b, y_c,
     sa, ra, sya, rya, sb, rb, szb, rzb,
-    ga, gb, vs, vr, us, ur, hx, scs, scr, scc,
+    ga, gb, vs, vr, us, ur, hq, scs, scr, scc, scx,
     sem_sa, sem_ra, sem_sya, sem_rya, sem_sb, sem_rb, sem_szb, sem_rzb,
     sem_gs, sem_ga, sem_gay, sem_gb, sem_gby,
-    sem_vs, sem_vr, sem_us, sem_ur, sem_hs, sem_hr, sem_cs, sem_cr,
+    sem_vs, sem_vr, sem_us, sem_ur, sem_uc, sem_hs, sem_hr, sem_cs, sem_cr,
 ):
     z, y, x, c = (lax.axis_index(name) for name in AXES)
     t = z * NY + y
@@ -92,9 +100,10 @@
     pending = []
 
     def send(src, dst, ssem, rsem, **device):
-        copy = rcopy(src, dst, ssem, rsem, **device)
-        copy.start()
-        pending.append(copy)
+        rcopy(src, dst, ssem, rsem, **device).start()
+
+    def sent(ref, sem):
+        pending.append(rcopy(ref, ref, sem, sem, c=other))
 
     def arrived(dst, ssem, rsem, **device):
         rcopy(dst, dst, ssem, rsem, **device).wait_recv()
@@ -108,10 +117,24 @@
     for peer in peers:
         pl.semaphore_signal(barrier, inc=1, device_id=peer, device_id_type=MESH)
 
+    row = lax.broadcasted_iota(I32, (BAND, BAND), 0)
+    col = lax.broadcasted_iota(I32, (BAND, BAND), 1)
+    for b in range(2):
+        on = (gaps[b : b + 1, :] == 1) & (col[0:1] + b * BAND < counts[0])
+        wm[b * BAND : (b + 1) * BAND] = jnp.broadcast_to(jnp.where(on, 1.0, 0.0), (BAND, BAND)).T
+
+    for b in range(2):
+        hq[0, 1 + b] = enc_v(wm[b * BAND : (b + 1) * BAND] * obs[b * BAND : (b + 1) * BAND])
+    pl.semaphore_wait(barrier, len(peers))
+    for place, goal, step in ((2, 0, t_up), (1, 3, t_down)):
+        send(
+            hq.at[0, place], hq.at[0, goal], sem_hs.at[0, goal], sem_hr.at[0, goal],
+            z=lax.div(step, NY), y=lax.rem(step, NY),
+        )
+        sent(hq.at[0, place], sem_hs.at[0, goal])
+
     keep_first = jnp.where(t == 0, 0.0, 1.0).astype(F32)
     keep_last = jnp.where(t == NZ * NY - 1, 0.0, 1.0).astype(F32)
-    row = lax.broadcasted_iota(I32, (BAND, BAND), 0)
-    col = lax.broadcasted_iota(I32, (BAND, BAND), 1)
     rolled = pltpu.roll(jnp.broadcast_to(taps[...], (BAND, BAND)), 0, 1, stride=1, stride_axis=0)
     lot = jnp.where(col >= row, rolled, 0.0)
     upt = jnp.where(col < row, rolled, 0.0)
@@ -129,10 +152,6 @@
     bm[BAND:, 2 * BAND : 3 * BAND] = ll + keep_last * uu
     bm[BAND:, 3 * BAND :] = keep_last * ul
 
-    for b in range(2):
-        on = (gaps[b : b + 1, :] == 1) & (col[0:1] + b * BAND < counts[0])
-        wm[b * BAND : (b + 1) * BAND] = jnp.broadcast_to(jnp.where(on, 1.0, 0.0), (BAND, BAND)).T
-
     line = lax.div(t * OWN, LANES)
     shift = t * OWN - line * LANES
     for diag, part_a, part_b in ((kaula, kda, kdb), (precond, pca, pcb)):
@@ -172,94 +191,117 @@
             gb[it, yy, zz, RB:] = jnp.zeros((LANES - RB, LANES), BF16)
         return carry
 
-    lax.fori_loop(0, NZ * NY, put_rows, 0)
-
     def at_a(target):
         return ata[target].reshape(NY * RA, 2 * BAND)
 
     def at_b(target):
         return atb[target].reshape(NZ * RB, 2 * BAND)
 
+    lax.fori_loop(0, NZ * NY, put_rows, 0)
+
     def filtered(st):
-        ext = hx[st].reshape(4 * BAND, BAND)
-        return (wm[...] * dot(bm[...], ext, HIGH)).astype(BF16)
+        ext = dec_v(hq[st])
+        w = (wm[...] * dot(bm[...], ext.reshape(4 * BAND, BAND), HIGH)).astype(BF16)
+        inner = ext[1] * w[0:BAND].astype(F32) + ext[2] * w[BAND:].astype(F32)
+        return w, jnp.sum(inner, 0, keepdims=True)
 
     def small_start(i, block):
         scs[i, 0] = block
         for k in range(1, NY):
-            send(scs.at[i, 0], scr.at[i, k], sem_cs.at[i, k], sem_cr.at[i, k], y=yp[k])
+            send(scs.at[i, 0], scr.at[i, k], sem_cs.at[i, 0], sem_cr.at[i, k], y=yp[k])
 
     def small_middle(i):
+        sent(scr.at[i, pl.ds(0, NY - 1)], sem_cs.at[i, 0])
         total = scs[i, 0]
         for k in range(1, NY):
-            arrived(scr.at[i, k], sem_cs.at[i, k], sem_cr.at[i, k], y=yp[k])
+            arrived(scr.at[i, k], sem_cs.at[i, 0], sem_cr.at[i, k], y=yp[k])
             total = total + scr[i, k]
         scs[i, 1] = total
         for k in range(1, NZ):
-            send(scs.at[i, 1], scr.at[i, NY + k], sem_cs.at[i, NY + k], sem_cr.at[i, NY + k], z=zp[k])
+            send(scs.at[i, 1], scr.at[i, NY + k], sem_cs.at[i, 1], sem_cr.at[i, NY + k], z=zp[k])
 
     def small_end(i):
+        sent(scr.at[i, pl.ds(0, NZ - 1)], sem_cs.at[i, 1])
         total = scs[i, 1]
         for k in range(1, NZ):
-            arrived(scr.at[i, NY + k], sem_cs.at[i, NY + k], sem_cr.at[i, NY + k], z=zp[k])
+            arrived(scr.at[i, NY + k], sem_cs.at[i, 1], sem_cr.at[i, NY + k], z=zp[k])
             total = total + scr[i, NY + k]
         return total
 
     half = NZ // 2 * RB
 
-    def scatter(st, w, early, late):
+    def long_way(j):
+        return 0 if j in (0, 3) else 1
+
+    def hops(way, j):
+        return NZ // 2 if long_way(j) == way else NZ // 2 - 1
+
+    def scatter(st, w, early, late, fill):
+        ways_y = ((0, yp[1]), (1, ym[1]))
+
+        def send_b(way, kind, peer):
+            send(sb.at[st, way, kind], rb.at[st, way, kind], sem_sb.at[st], sem_rb.at[way, kind], y=peer)
+
+        def got_b(way, kind):
+            arrived(rb.at[st, way, kind], sem_sb.at[st], sem_rb.at[way, kind], y=yp[1])
+
+        def send_a(way, s, j):
+            send(
+                sa.at[st, way, s, j], ra.at[st, way, s, j], sem_sa.at[st, way, abs(long_way(j) - way)],
+                sem_ra.at[way, s, j], z=zp[1] if way == 0 else zm[1],
+            )
+
+        def got_a(way, s, j):
+            arrived(ra.at[st, way, s, j], sem_sa.at[st, way, 0], sem_ra.at[way, s, j], z=zp[1])
+
         part = dot(at_b(yp[2]), w).reshape(2, NZ // 2, RB, 128)
-        for way, peer in ((0, yp[1]), (1, ym[1])):
+        for way, peer in ways_y:
             sb[st, way, 0] = enc_b(part[way])
-            send(sb.at[st, way, 0], rb.at[st, way, 0], sem_sb.at[st, way, 0], sem_rb.at[st, way, 0], y=peer)
-        for way, target, peer in ((0, zp[4], zp[1]), (1, zm[3], zm[1])):
-            sa[st, way, 0] = enc_a(dot(at_a(target), w).reshape(NY, RA, 128))
+            send_b(way, 0, peer)
+        far = enc_a(dot(at_a(zp[4]), w).reshape(NY, RA, 128))
+        for j in range(NY):
+            sa[st, long_way(j), 0, j] = far[j]
+            send_a(long_way(j), 0, j)
+        for way, target in ((0, zp[3]), (1, zm[3])):
+            near = dot(at_a(target), w).reshape(NY, RA, 128)
+            y_a[target] = near
             for j in range(NY):
-                send(
-                    sa.at[st, way, 0, j], ra.at[st, way, 0, j],
-                    sem_sa.at[st, way, 0, j], sem_ra.at[st, way, 0, j], z=peer,
-                )
-        for way, peer in ((0, yp[1]), (1, ym[1])):
+                if long_way(j) != way:
+                    sa[st, way, 0, j] = enc_a(near[j])
+                    send_a(way, 0, j)
+        for way, peer in ways_y:
             part = dot(at_b(peer), w).reshape(2, NZ // 2, RB, 128)
             sb[st, way, 1] = enc_b(part[1 - way])
-            send(sb.at[st, way, 1], rb.at[st, way, 1], sem_sb.at[st, way, 1], sem_rb.at[st, way, 1], y=peer)
+            send_b(way, 1, peer)
             y_c[way] = part[way]
 
         def product(i, carry):
-            target = lax.rem(z + 5 + i, NZ)
+            target = lax.rem(z + NZ - 2 + i, NZ)
             y_a[target] = dot(at_a(target), w).reshape(NY, RA, 128)
             return carry
 
-        lax.fori_loop(1, NZ - 1, product, 0)
+        lax.fori_loop(0, 5, product, 0)
         y_b[...] = dot(at_b(y), w).reshape(NZ, RB, 128)
         early()
         for s in range(1, 4):
-            for j in range(NY):
-                for way, target, peer in ((0, zp[4 - s], zp[1]), (1, zm[3 - s], zm[1])):
-                    if way == 1 and s == 3:
-                        continue
-                    arrived(
-                        ra.at[st, way, s - 1, j], sem_sa.at[st, way, s - 1, j], sem_ra.at[st, way, s - 1, j], z=peer
-                    )
-                    sa[st, way, s, j] = enc_a(dec_a(ra[st, way, s - 1, j]) + y_a[target, j])
-                    send(
-                        sa.at[st, way, s, j], ra.at[st, way, s, j],
-                        sem_sa.at[st, way, s, j], sem_ra.at[st, way, s, j], z=peer,
-                    )
+            for j in (0, 3, 1, 2):
+                for way in (long_way(j), 1 - long_way(j)):
+                    if s < hops(way, j):
+                        got_a(way, s - 1, j)
+                        target = zp[hops(way, j) - s] if way == 0 else zm[hops(way, j) - s]
+                        sa[st, way, s, j] = enc_a(dec_a(ra[st, way, s - 1, j]) + y_a[target, j])
+                        send_a(way, s, j)
+                fill((s - 1) * NY + j)
             if s == 1:
-                for way, peer in ((0, yp[1]), (1, ym[1])):
-                    arrived(rb.at[st, way, 0], sem_sb.at[st, way, 0], sem_rb.at[st, way, 0], y=peer)
+                for way, peer in ways_y:
+                    got_b(way, 0)
                     sb[st, way, 2] = enc_b(y_c[way] + dec_b(rb[st, way, 0]))
-                    send(
-                        sb.at[st, way, 2], rb.at[st, way, 2], sem_sb.at[st, way, 2], sem_rb.at[st, way, 2], y=peer
-                    )
+                    send_b(way, 2, peer)
                 late()
             if s == 2:
-                for way, peer in ((0, yp[1]), (1, ym[1])):
+                for way, peer in ways_y:
                     for kind in (1, 2):
-                        arrived(
-                            rb.at[st, way, kind], sem_sb.at[st, way, kind], sem_rb.at[st, way, kind], y=peer
-                        )
+                        got_b(way, kind)
                 low = y_b[0 : NZ // 2] + dec_b(rb[st, 0, 2]) + dec_b(rb[st, 1, 1])
                 y_b[0 : NZ // 2] = low
                 szb[st, 0 : NZ // 2] = enc_b(low)
@@ -267,23 +309,29 @@
                 y_b[NZ // 2 :] = high
                 szb[st, NZ // 2 :] = enc_b(high)
                 for k in (4, 3, 5, 2, 6, 1, 7):
-                    send(szb.at[st, zp[k]], rzb.at[st, k], sem_szb.at[st, k], sem_rzb.at[st, k], z=zp[k])
-        for j in range(NY):
-            arrived(ra.at[st, 0, 3, j], sem_sa.at[st, 0, 3, j], sem_ra.at[st, 0, 3, j], z=zp[1])
-            arrived(ra.at[st, 1, 2, j], sem_sa.at[st, 1, 2, j], sem_ra.at[st, 1, 2, j], z=zm[1])
-            total = dec_a(ra[st, 0, 3, j]) + dec_a(ra[st, 1, 2, j]) + y_a[z, j]
+                    send(szb.at[st, zp[k]], rzb.at[st, k], sem_szb.at[st], sem_rzb.at[k], z=zp[k])
+        for j in (0, 3, 1, 2):
+            for way in range(2):
+                got_a(way, hops(way, j) - 1, j)
+            total = dec_a(ra[st, 0, hops(0, j) - 1, j]) + dec_a(ra[st, 1, hops(1, j) - 1, j]) + y_a[z, j]
             y_a[z, j] = total
             sya[st, j] = enc_a(total)
         for k in (2, 1, 3):
-            send(sya.at[st, yp[k]], rya.at[st, k], sem_sya.at[st, k], sem_rya.at[st, k], y=yp[k])
+            send(sya.at[st, yp[k]], rya.at[st, k], sem_sya.at[st], sem_rya.at[k], y=yp[k])
         sum_b = y_b[z]
         for k in range(1, NZ):
-            arrived(rzb.at[st, k], sem_szb.at[st, k], sem_rzb.at[st, k], z=zp[k])
+            arrived(rzb.at[st, k], sem_szb.at[st], sem_rzb.at[k], z=zp[k])
             sum_b = sum_b + dec_b(rzb[st, k])
         sum_a = y_a[z, y]
         for k in range(1, NY):
-            arrived(rya.at[st, k], sem_sya.at[st, k], sem_rya.at[st, k], y=yp[k])
+            arrived(rya.at[st, k], sem_sya.at[st], sem_rya.at[k], y=yp[k])
             sum_a = sum_a + dec_a(rya[st, k])
+        for way in range(2):
+            sent(sa.at[st, way, :, pl.ds(0, 2)], sem_sa.at[st, way, 0])
+            sent(sa.at[st, way, pl.ds(0, 3), pl.ds(0, 2)], sem_sa.at[st, way, 1])
+        sent(sb.at[st], sem_sb.at[st])
+        sent(szb.at[st, pl.ds(0, NZ - 1)], sem_szb.at[st])
+        sent(sya.at[st, pl.ds(0, NY - 1)], sem_sya.at[st])
         return sum_a, sum_b
 
     first_half, second_half = (0, 1, 7, 2), (6, 3, 5, 4)
@@ -299,49 +347,53 @@
             return gb.at[it, yy, zz, pl.ds(0, RB)]
 
         def put_a(way, s, k):
-            zz, yy = (zm[s] if way == 0 else zp[s]), ym[k]
-            peer = zp[1] if way == 0 else zm[1]
-            send(part_a(it, zz, yy), part_a(it, zz, yy), sem_gs.at[it, 0, way, s, k], sem_ga.at[it, way, s, k], z=peer)
+            block = part_a(it, zm[s] if way == 0 else zp[s], ym[k])
+            send(block, block, sem_gs.at[it, 0], sem_ga.at[way, s, k], z=zp[1] if way == 0 else zm[1])
 
         def got_a(way, s, k):
-            zz, yy = (zm[s + 1] if way == 0 else zp[s + 1]), ym[k]
-            arrived(part_a(it, zz, yy), sem_gs.at[it, 0, way, s, k], sem_ga.at[it, way, s, k], z=zp[1])
+            block = part_a(it, zm[s + 1] if way == 0 else zp[s + 1], ym[k])
+            arrived(block, sem_gs.at[it, 0], sem_ga.at[way, s, k], z=zp[1])
 
         def put_b(way, s, k):
-            zz, yy = zm[k], (ym[s] if way == 0 else yp[s])
-            peer = yp[1] if way == 0 else ym[1]
-            send(part_b(it, yy, zz), part_b(it, yy, zz), sem_gs.at[it, 1, way, s, k], sem_gby.at[it, way, s, k], y=peer)
+            block = part_b(it, ym[s] if way == 0 else yp[s], zm[k])
+            send(block, block, sem_gs.at[it, 1], sem_gby.at[way, s, k], y=yp[1] if way == 0 else ym[1])
 
         def got_b(way, s, k):
-            zz, yy = zm[k], (ym[s + 1] if way == 0 else yp[s + 1])
-            arrived(part_b(it, yy, zz), sem_gs.at[it, 1, way, s, k], sem_gby.at[it, way, s, k], y=yp[1])
-
+            block = part_b(it, ym[s + 1] if way == 0 else yp[s + 1], zm[k])
+            arrived(block, sem_gs.at[it, 1], sem_gby.at[way, s, k], y=yp[1])
+
+        def from_z(k):
+            arrived(part_b(it, y, zm[k]), sem_gs.at[it, 3], sem_gb.at[k], z=zp[k])
+            if k == 5:
+                send(part_b(it, y, zm[5]), part_b(it, y, zm[5]), sem_gs.at[it, 3], sem_gb.at[4], z=zm[1])
+            put_b(0, 0, k)
+            put_b(1, 0, k)
+
+        own_a, own_b = part_a(it, z, y), part_b(it, y, z)
         for k in (2, 1, 3):
-            send(part_a(it, z, y), part_a(it, z, y), sem_gs.at[it, 0, 0, 4, k], sem_gay.at[it, k], y=yp[k])
+            send(own_a, own_a, sem_gs.at[it, 2], sem_gay.at[k], y=yp[k])
         put_a(0, 0, 0)
         put_a(1, 0, 0)
-        for k in (4, 3, 5, 2, 6, 1, 7):
-            send(part_b(it, y, z), part_b(it, y, z), sem_gs.at[it, 1, 0, 2, k], sem_gb.at[it, k], z=zp[k])
+        for k in (5, 3, 2, 6, 1, 7):
+            send(own_b, own_b, sem_gs.at[it, 3], sem_gb.at[k], z=zp[k])
         put_b(0, 0, 0)
         put_b(1, 0, 0)
         for k in (1, 3, 2):
-            arrived(part_a(it, z, ym[k]), sem_gs.at[it, 0, 0, 4, k], sem_gay.at[it, k], y=yp[k])
+            arrived(part_a(it, z, ym[k]), sem_gs.at[it, 2], sem_gay.at[k], y=yp[k])
             put_a(0, 0, k)
             put_a(1, 0, k)
         v = dot(aa[z], ga[it, z].reshape(NY * LANES, LANES))
         for s in range(1, 4):
             for k in (0, 1, 3, 2):
-                got_a(0, s - 1, k)
-                put_a(0, s, k)
-                got_a(1, s - 1, k)
-                if s < 3:
-                    put_a(1, s, k)
+                for way in (long_way(k), 1 - long_way(k)):
+                    got_a(way, s - 1, k)
+                    if s < hops(way, k):
+                        put_a(way, s, k)
             if s == 1:
-                for k in (1, 7, 2, 6, 3, 5, 4):
-                    arrived(part_b(it, y, zm[k]), sem_gs.at[it, 1, 0, 2, k], sem_gb.at[it, k], z=zp[k])
-                    put_b(0, 0, k)
-                    put_b(1, 0, k)
+                for k in (1, 7, 2, 6, 5, 3):
+                    from_z(k)
             if s == 2:
+                from_z(4)
                 for k in first_half:
                     got_b(0, 0, k)
                     put_b(0, 1, k)
@@ -364,7 +416,11 @@
             got_b(1, 1, k)
         v = v + dot(ab[yp[2]], gb[it, yp[2]].reshape(NZ * LANES, LANES))
         for k in range(NY):
-            got_a(0, 3, k)
+            got_a(long_way(k), 3, k)
+        sent(ga.at[it, pl.ds(0, NZ - 1), :, pl.ds(0, RA)], sem_gs.at[it, 0])
+        sent(gb.at[it, pl.ds(0, NY - 1), :, pl.ds(0, RB)], sem_gs.at[it, 1])
+        sent(ga.at[it, 0, pl.ds(0, NY - 1), pl.ds(0, RA)], sem_gs.at[it, 2])
+        sent(gb.at[it, 0, pl.ds(0, NZ - 1), pl.ds(0, RB)], sem_gs.at[it, 3])
         return v + dot(aa[zm[4]], ga[it, zm[4]].reshape(NY * LANES, LANES))
 
     def slab_values(it, v, scal, finish):
@@ -373,47 +429,53 @@
         send(vs.at[it, other], vr.at[it], sem_vs.at[it, 0], sem_vr.at[it, 0], c=other)
         send(scc.at[it, 0], scc.at[it, 1], sem_vs.at[it, 1], sem_vr.at[it, 1], c=other)
         arrived(vr.at[it], sem_vs.at[it, 0], sem_vr.at[it, 0], c=other)
+        chip = vs[it, c] + vr[it]
+        us[it] = enc_v(chip)
+        for k in (2, 1, 3):
+            send(us.at[it], ur.at[it, k], sem_us.at[it, 0], sem_ur.at[it, k], x=xp[k])
         arrived(scc.at[it, 1], sem_vs.at[it, 1], sem_vr.at[it, 1], c=other)
-        us[it, 0:BAND] = vs[it, c] + vr[it]
-        us[it, BAND:] = scc[it, 0] + scc[it, 1]
+        scal = scc[it, 0] + scc[it, 1]
+        scx[it, 0] = scal
         for k in (2, 1, 3):
-            send(us.at[it], ur.at[it, k], sem_us.at[it, k], sem_ur.at[it, k], x=xp[k])
-        total = us[it]
+            send(scx.at[it, 0], scx.at[it, k], sem_us.at[it, 1], sem_uc.at[it, k], x=xp[k])
         for k in range(1, NX):
-            arrived(ur.at[it, k], sem_us.at[it, k], sem_ur.at[it, k], x=xp[k])
-            total = total + ur[it, k]
+            arrived(ur.at[it, k], sem_us.at[it, 0], sem_ur.at[it, k], x=xp[k])
+            chip = chip + dec_v(ur[it, k])
+            arrived(scx.at[it, k], sem_us.at[it, 1], sem_uc.at[it, k], x=xp[k])
+            scal = scal + scx[it, k]
         mask = wm[pl.ds(pl.multiple_of(c * BAND, BAND), BAND), :]
-        block, scal = finish(mask * total[0:BAND], total[BAND:])
-        hx[it + 1, 1 + c] = block
+        block, scal = finish(mask * chip, scal)
+        hq[it + 1, 1 + c] = enc_v(block)
         slot = 3 - 3 * c
         step = jnp.where(c == 0, t_down, t_up)
-        mine = hx.at[it + 1, 1 + c]
-        send(mine, mine, sem_hs.at[it + 1, 1 + c], sem_hr.at[it + 1, 1 + c], c=other)
+        mine = hq.at[it + 1, 1 + c]
         for core in range(NC):
             send(
-                mine, hx.at[it + 1, slot], sem_hs.at[it + 1, 4 + core], sem_hr.at[it + 1, slot],
+                mine, hq.at[it + 1, slot], sem_hs.at[it + 1, 1 + core], sem_hr.at[it + 1, slot],
                 z=lax.div(step, NY), y=lax.rem(step, NY), c=jnp.int32(core),
             )
+        send(mine, mine, sem_hs.at[it + 1, 0], sem_hr.at[it + 1, 1 + c], c=other)
+        for k in range(3):
+            sent(mine, sem_hs.at[it + 1, k])
+        sent(vs.at[it, 0], sem_vs.at[it, 0])
+        sent(scc.at[it, 0], sem_vs.at[it, 1])
+        sent(ur.at[it, pl.ds(0, NX - 1)], sem_us.at[it, 0])
+        sent(scx.at[it, pl.ds(0, NX - 1)], sem_us.at[it, 1])
         for place in (2 - c, 0, 3):
-            arrived(hx.at[it + 1, place], sem_hs.at[it + 1, 0], sem_hr.at[it + 1, place], c=other)
+            arrived(hq.at[it + 1, place], sem_hs.at[it + 1, 0], sem_hr.at[it + 1, place], c=other)
         return block, scal
 
-    masked = wm[...] * obs[...]
-    hx[0, 1] = masked[0:BAND]
-    hx[0, 2] = masked[BAND:]
-    pl.semaphore_wait(barrier, len(peers))
-    send(
-        hx.at[0, 2], hx.at[0, 0], sem_hs.at[0, 0], sem_hr.at[0, 0],
-        z=lax.div(t_up, NY), y=lax.rem(t_up, NY),
-    )
-    send(
-        hx.at[0, 1], hx.at[0, 3], sem_hs.at[0, 3], sem_hr.at[0, 3],
-        z=lax.div(t_down, NY), y=lax.rem(t_down, NY),
-    )
-    arrived(hx.at[0, 0], sem_hs.at[0, 0], sem_hr.at[0, 0], c=other)
-    arrived(hx.at[0, 3], sem_hs.at[0, 3], sem_hr.at[0, 3], c=other)
-    nothing = lambda: None
-    res_a, res_b = scatter(0, filtered(0), lambda: lax.fori_loop(0, NZ * NY, put_columns, 0), nothing)
+    arrived(hq.at[0, 0], sem_hs.at[0, 0], sem_hr.at[0, 0], c=other)
+    arrived(hq.at[0, 3], sem_hs.at[0, 0], sem_hr.at[0, 3], c=other)
+
+    def nothing(*_):
+        return None
+
+    def some_columns(i):
+        lax.fori_loop(3 * i, min(3 * i + 3, NZ * NY), put_columns, 0)
+
+    w, _ = filtered(0)
+    res_a, res_b = scatter(0, w, nothing, nothing, some_columns)
 
     def col_sum(a, b):
         return jnp.sum(a, 0, keepdims=True) + jnp.sum(b, 0, keepdims=True)
@@ -428,12 +490,8 @@
     block, scal = slab_values(0, v, small_end(0), lambda block, scal: (block, scal))
     norm, diag = scal[0:1], scal[1:2]
 
-    def slab_inner(it, w):
-        own = hx[it + 1, 1] * w[0:BAND].astype(F32) + hx[it + 1, 2] * w[BAND:].astype(F32)
-        return rows_of(jnp.sum(own, 0, keepdims=True))
-
-    w = filtered(1)
-    image_a, image_b = scatter(1, w, lambda: small_start(1, slab_inner(0, w)), lambda: small_middle(1))
+    w, inner = filtered(1)
+    image_a, image_b = scatter(1, w, lambda: small_start(1, rows_of(inner)), lambda: small_middle(1), nothing)
     step_len = norm / (diag + small_end(1)[0:1])
     image_a, image_b = image_a + kda[...] * dir_a, image_b + kdb[...] * dir_b
     sol_a, sol_b = step_len * dir_a, step_len * dir_b
@@ -458,8 +516,8 @@
     norm = scal[0:1]
     diag = scal[1:2] + 2.0 * ratio * scal[2:3] + ratio * ratio * diag
     dir_a, dir_b = scaled_a + ratio * dir_a, scaled_b + ratio * dir_b
-    w = filtered(2)
-    image_a, image_b = scatter(2, w, lambda: small_start(3, slab_inner(1, w)), lambda: small_middle(3))
+    w, last_inner = filtered(2)
+    image_a, image_b = scatter(2, w, lambda: small_start(3, rows_of(last_inner)), lambda: small_middle(3), nothing)
     step_len = norm / (diag + small_end(3)[0:1])
     image_a, image_b = image_a + kda[...] * dir_a, image_b + kdb[...] * dir_b
     sol_a, sol_b = sol_a + step_len * dir_a, sol_b + step_len * dir_b
@@ -505,17 +563,18 @@
         vm((2, NY, NZ, LANES, LANES), BF16),
         vm((2, 2, BAND, 128), F32),
         vm((2, BAND, 128), F32),
-        vm((2, BAND + 8, 128), F32),
-        vm((2, NX, BAND + 8, 128), F32),
-        vm((3, 4, BAND, 128), F32),
+        vm((2, BAND + 16, 128), I16),
+        vm((2, NX, BAND + 16, 128), I16),
+        vm((3, 4, BAND + 16, 128), I16),
         vm((4, 2, 8, 128), F32),
         vm((4, NY + NZ, 8, 128), F32),
         vm((2, 2, 8, 128), F32),
-        dma((3, 2, 4, NY)), dma((3, 2, 4, NY)), dma((3, NY)), dma((3, NY)),
-        dma((3, 2, 3)), dma((3, 2, 3)), dma((3, NZ)), dma((3, NZ)),
-        dma((2, 2, 2, 5, NZ)), dma((2, 2, 4, NY)), dma((2, NY)), dma((2, NZ)), dma((2, 2, 2, NZ)),
-        dma((2, 2)), dma((2, 2)), dma((2, NX)), dma((2, NX)), dma((3, 6)), dma((3, 4)),
-        dma((4, NY + NZ)), dma((4, NY + NZ)),
+        vm((2, NX, 8, 128), F32),
+        dma((3, 2, 2)), dma((2, 4, NY)), dma((3,)), dma((NY,)),
+        dma((3,)), dma((2, 3)), dma((3,)), dma((NZ,)),
+        dma((2, 4)), dma((2, 4, NY)), dma((NY,)), dma((NZ,)), dma((2, 2, NZ)),
+        dma((2, 2)), dma((2, 2)), dma((2, 2)), dma((2, NX)), dma((2, NX)), dma((3, 4)), dma((3, 4)),
+        dma((4, 2)), dma((4, NY + NZ)),
     ]
     out = jax.ShapeDtypeStruct((OWN, LANES), F32)
     return pl.pallas_call(

time: 174 us -> 155 us (0.89)
  Pallas kernels: 169 us -> 151 us
    pallas_call x1, Pallas kernels: 169 us -> 151 us  [shards(): pl.pallas_call(kernel, name='cg', out_shape=(out, out), in_specs=[pl.Bloc...]
where the time goes in v3:
time: 155 us
  Pallas kernels  151 us (97%)
  local copies, waits for them, and re-layouts  3.09 us (2%)
    pallas_call x1, Pallas kernels, shards(): pl.pallas_call(kernel, name='cg', out_shape=(out, out), in_specs=[pl.Bloc...  151 us

profile of v3, /device:TPU:1, one launch (start us, length us, event | category | flops | bytes accessed | tf_op | source)
XLA Modules:
  0.0 155.1 jit_solution(2925621279458933710)
XLA Ops:
  1.3 150.7 %cg.1 = (f32[196,128]{1,0:T(8,128)}, f32[196,128]{1,0:T(8,128)}) custom-call(bf16[256,6272]{1,0:T(8,128)(2,1)} %design.1, f32[256,128]{1,0:T(8,128)} %obs.1, s32[1]{0:T(128)S(6)} %copy.11.counts, s32[2,128]{1,0:T(2,128)} %bitcast.6, f32[1,128]{1,0:T(1,128)} %bitcast.7, f32[49,128]{1,0:T(8,128)} %bitcast.4, f32[49,128]{1,0:T(8,128)} %bitcast.5), custom_call_target="tpu_custom_call" | custom-call | tf_op jit(solution)/shard_map/cg/pallas_call | solution.py:580
  152.0 1.5 copy.12
  153.6 1.5 copy.13

commit v4 on v3

--- a/solution.py
+++ b/solution.py
@@ -13,8 +13,8 @@
 COEF = ("x", "c")
 MESH = pl.DeviceIdType.MESH
 NZ, NY, NX, NC = 8, 4, 4, 2
-NA, NB = 92, 104
-RA, RB = 96, 112
+NA, NB = 104, 92
+RA, RB = 112, 96
 OWN = NA + NB
 LANES = 128
 WIDE = 3 * LANES
@@ -34,17 +34,27 @@
     return lax.dot_general(a, b, (((1,), (1,)), ((), ())), preferred_element_type=F32, precision=precision)
 
 
+def split(v):
+    high = v.astype(BF16)
+    return high, (v - high.astype(F32)).astype(BF16)
+
+
+HEADROOM = 0.998
+
+
 def encoded(v, spare):
+    tail = v.shape[-2] - 8
     top = jnp.maximum(jnp.max(jnp.abs(v), axis=-2, keepdims=True), 1e-30)
     power = jnp.floor(jnp.log2(top)) + 1.0
-    q = jnp.clip(jnp.round(v * jnp.exp2(15.0 - power)), -32767.0, 32767.0)
-    row = lax.broadcasted_iota(I32, v.shape, v.ndim - 2)
-    return jnp.where(row == spare, power, q).astype(I32).astype(I16)
+    q = jnp.round(v * (jnp.exp2(15.0 - power) * HEADROOM))
+    row = lax.broadcasted_iota(I32, (*v.shape[:-2], 8, v.shape[-1]), v.ndim - 2)
+    last = jnp.where(row == spare - tail, power, q[..., tail:, :])
+    return jnp.concatenate([q[..., :tail, :], last], -2).astype(I32).astype(I16)
 
 
 def decoded(q, spare):
     v = q.astype(I32).astype(F32)
-    return v * jnp.exp2(v[..., spare : spare + 1, :] - 15.0)
+    return v * (jnp.exp2(v[..., spare : spare + 1, :] - 15.0) * (1.0 / HEADROOM))
 
 
 def enc_a(v):
@@ -64,11 +74,11 @@
 
 
 def enc_v(v):
-    return encoded(jnp.concatenate([v, jnp.zeros((16, LANES), F32)], 0), BAND)
+    return encoded(jnp.concatenate([v, jnp.zeros((16, LANES), F32)], 0), BAND + 8)
 
 
 def dec_v(q):
-    return decoded(q, BAND)[..., 0:BAND, :]
+    return decoded(q, BAND + 8)[..., 0:BAND, :]
 
 
 def rcopy(src, dst, ssem, rsem, **device):
@@ -80,7 +90,7 @@
 def kernel(
     design, obs, counts, gaps, taps, kaula, precond,
     xout, rout,
-    aa, ab, ata, atb, wm, kda, kdb, pca, pcb, column, bm, y_a, y_b, y_c,
+    aa, ab, ata, atb, wm, kda, kdb, pca, pcb, column, bm, bm_high, bm_low, y_a, y_b, y_c,
     sa, ra, sya, rya, sb, rb, szb, rzb,
     ga, gb, vs, vr, us, ur, hq, scs, scr, scc, scx,
     sem_sa, sem_ra, sem_sya, sem_rya, sem_sb, sem_rb, sem_szb, sem_rzb,
@@ -125,6 +135,42 @@
 
     for b in range(2):
         hq[0, 1 + b] = enc_v(wm[b * BAND : (b + 1) * BAND] * obs[b * BAND : (b + 1) * BAND])
+    def picked(p):
+        first = jnp.minimum(lax.div(p * OWN, LANES), design.shape[1] // LANES - 3)
+        window = design[:, pl.ds(pl.multiple_of(first * LANES, LANES), WIDE)]
+        place = lax.broadcasted_iota(I32, (2 * LANES, WIDE), 0)
+        wanted = jnp.where(place < LANES, place, place - LANES + NA)
+        real = ((place < NA) | (place >= LANES)) & (place < LANES + NB)
+        at = lax.broadcasted_iota(I32, (2 * LANES, WIDE), 1) - (p * OWN - first * LANES)
+        return window, jnp.where((at == wanted) & real, 1.0, 0.0).astype(BF16)
+
+    def put_rows(p, carry):
+        window, pick = picked(p)
+        rows = dot_t(pick, window).astype(BF16)
+        zz, yy = lax.div(p, NY), lax.rem(p, NY)
+        ata[zz, yy] = rows[0:RA]
+        atb[yy, zz] = rows[LANES : LANES + RB]
+        return carry
+
+    def put_columns(p, carry):
+        window, pick = picked(p)
+        columns = dot_t(window, pick).astype(BF16)
+        zz, yy = lax.div(p, NY), lax.rem(p, NY)
+        aa[zz, :, pl.ds(pl.multiple_of(yy * LANES, LANES), LANES)] = columns[:, 0:LANES]
+        ab[yy, :, pl.ds(pl.multiple_of(zz * LANES, LANES), LANES)] = columns[:, LANES:]
+        for it in range(2):
+            ga[it, zz, yy, RA:] = jnp.zeros((LANES - RA, LANES), BF16)
+            gb[it, yy, zz, RB:] = jnp.zeros((LANES - RB, LANES), BF16)
+        return carry
+
+    def at_a(target):
+        return ata[target].reshape(NY * RA, 2 * BAND)
+
+    def at_b(target):
+        return atb[target].reshape(NZ * RB, 2 * BAND)
+
+    early_rows = 16
+    lax.fori_loop(0, early_rows, put_rows, 0)
     pl.semaphore_wait(barrier, len(peers))
     for place, goal, step in ((2, 0, t_up), (1, 3, t_down)):
         send(
@@ -151,6 +197,7 @@
     bm[BAND:, BAND : 2 * BAND] = lu
     bm[BAND:, 2 * BAND : 3 * BAND] = ll + keep_last * uu
     bm[BAND:, 3 * BAND :] = keep_last * ul
+    bm_high[...], bm_low[...] = split(bm[...])
 
     line = lax.div(t * OWN, LANES)
     shift = t * OWN - line * LANES
@@ -163,45 +210,13 @@
         part_a[...] = jnp.where(row_a < NA, column[pl.ds(shift, RA), :], 0.0)
         part_b[...] = jnp.where(row_b < NB, column[pl.ds(shift + NA, RB), :], 0.0)
 
-    def picked(p):
-        first = jnp.minimum(lax.div(p * OWN, LANES), design.shape[1] // LANES - 3)
-        window = design[:, pl.ds(pl.multiple_of(first * LANES, LANES), WIDE)]
-        place = lax.broadcasted_iota(I32, (2 * LANES, WIDE), 0)
-        wanted = jnp.where(place < LANES, place, place - LANES + NA)
-        real = ((place < NA) | (place >= LANES)) & (place < LANES + NB)
-        at = lax.broadcasted_iota(I32, (2 * LANES, WIDE), 1) - (p * OWN - first * LANES)
-        return window, jnp.where((at == wanted) & real, 1.0, 0.0).astype(BF16)
-
-    def put_rows(p, carry):
-        window, pick = picked(p)
-        rows = dot_t(pick, window).astype(BF16)
-        zz, yy = lax.div(p, NY), lax.rem(p, NY)
-        ata[zz, yy] = rows[0:RA]
-        atb[yy, zz] = rows[LANES : LANES + RB]
-        return carry
-
-    def put_columns(p, carry):
-        window, pick = picked(p)
-        columns = dot_t(window, pick).astype(BF16)
-        zz, yy = lax.div(p, NY), lax.rem(p, NY)
-        aa[zz, :, pl.ds(pl.multiple_of(yy * LANES, LANES), LANES)] = columns[:, 0:LANES]
-        ab[yy, :, pl.ds(pl.multiple_of(zz * LANES, LANES), LANES)] = columns[:, LANES:]
-        for it in range(2):
-            ga[it, zz, yy, RA:] = jnp.zeros((LANES - RA, LANES), BF16)
-            gb[it, yy, zz, RB:] = jnp.zeros((LANES - RB, LANES), BF16)
-        return carry
-
-    def at_a(target):
-        return ata[target].reshape(NY * RA, 2 * BAND)
-
-    def at_b(target):
-        return atb[target].reshape(NZ * RB, 2 * BAND)
-
-    lax.fori_loop(0, NZ * NY, put_rows, 0)
+    lax.fori_loop(early_rows, NZ * NY, put_rows, 0)
 
     def filtered(st):
         ext = dec_v(hq[st])
-        w = (wm[...] * dot(bm[...], ext.reshape(4 * BAND, BAND), HIGH)).astype(BF16)
+        high, low = split(ext.reshape(4 * BAND, BAND))
+        series = dot(bm_high[...], high) + (dot(bm_high[...], low) + dot(bm_low[...], high))
+        w = (wm[...] * series).astype(BF16)
         inner = ext[1] * w[0:BAND].astype(F32) + ext[2] * w[BAND:].astype(F32)
         return w, jnp.sum(inner, 0, keepdims=True)
 
@@ -233,8 +248,8 @@
     def long_way(j):
         return 0 if j in (0, 3) else 1
 
-    def hops(way, j):
-        return NZ // 2 if long_way(j) == way else NZ // 2 - 1
+    def along_z(way, links):
+        return zp[links] if way == 0 else zm[links]
 
     def scatter(st, w, early, late, fill):
         ways_y = ((0, yp[1]), (1, ym[1]))
@@ -248,7 +263,7 @@
         def send_a(way, s, j):
             send(
                 sa.at[st, way, s, j], ra.at[st, way, s, j], sem_sa.at[st, way, abs(long_way(j) - way)],
-                sem_ra.at[way, s, j], z=zp[1] if way == 0 else zm[1],
+                sem_ra.at[way, s, j], z=along_z(way, 2 if s == 0 else 1),
             )
 
         def got_a(way, s, j):
@@ -262,13 +277,10 @@
         for j in range(NY):
             sa[st, long_way(j), 0, j] = far[j]
             send_a(long_way(j), 0, j)
-        for way, target in ((0, zp[3]), (1, zm[3])):
-            near = dot(at_a(target), w).reshape(NY, RA, 128)
-            y_a[target] = near
+        for way in range(2):
+            sa[st, way, 1] = enc_a(dot(at_a(along_z(way, 3)), w).reshape(NY, RA, 128))
             for j in range(NY):
-                if long_way(j) != way:
-                    sa[st, way, 0, j] = enc_a(near[j])
-                    send_a(way, 0, j)
+                send_a(way, 1, j)
         for way, peer in ways_y:
             part = dot(at_b(peer), w).reshape(2, NZ // 2, RB, 128)
             sb[st, way, 1] = enc_b(part[1 - way])
@@ -283,37 +295,53 @@
         lax.fori_loop(0, 5, product, 0)
         y_b[...] = dot(at_b(y), w).reshape(NZ, RB, 128)
         early()
-        for s in range(1, 4):
-            for j in (0, 3, 1, 2):
-                for way in (long_way(j), 1 - long_way(j)):
-                    if s < hops(way, j):
-                        got_a(way, s - 1, j)
-                        target = zp[hops(way, j) - s] if way == 0 else zm[hops(way, j) - s]
-                        sa[st, way, s, j] = enc_a(dec_a(ra[st, way, s - 1, j]) + y_a[target, j])
-                        send_a(way, s, j)
-                fill((s - 1) * NY + j)
-            if s == 1:
-                for way, peer in ways_y:
-                    got_b(way, 0)
-                    sb[st, way, 2] = enc_b(y_c[way] + dec_b(rb[st, way, 0]))
-                    send_b(way, 2, peer)
-                late()
-            if s == 2:
-                for way, peer in ways_y:
-                    for kind in (1, 2):
-                        got_b(way, kind)
-                low = y_b[0 : NZ // 2] + dec_b(rb[st, 0, 2]) + dec_b(rb[st, 1, 1])
-                y_b[0 : NZ // 2] = low
-                szb[st, 0 : NZ // 2] = enc_b(low)
-                high = y_b[NZ // 2 :] + dec_b(rb[st, 0, 1]) + dec_b(rb[st, 1, 2])
-                y_b[NZ // 2 :] = high
-                szb[st, NZ // 2 :] = enc_b(high)
-                for k in (4, 3, 5, 2, 6, 1, 7):
-                    send(szb.at[st, zp[k]], rzb.at[st, k], sem_szb.at[st], sem_rzb.at[k], z=zp[k])
-        for j in (0, 3, 1, 2):
+        for i in range(3):
+            fill(i)
+
+        def pass_on(s, j):
+            codes = []
             for way in range(2):
-                got_a(way, hops(way, j) - 1, j)
-            total = dec_a(ra[st, 0, hops(0, j) - 1, j]) + dec_a(ra[st, 1, hops(1, j) - 1, j]) + y_a[z, j]
+                got_a(way, s - 1, j)
+                if s == 2 and way == long_way(j):
+                    got_a(way, 0, j)
+            for way in range(2):
+                total = dec_a(ra[st, way, s - 1, j]) + y_a[along_z(way, 4 - s), j]
+                if s == 2 and way == long_way(j):
+                    total = total + dec_a(ra[st, way, 0, j])
+                codes.append(enc_a(total))
+            for way in range(2):
+                sa[st, way, s, j] = codes[way]
+            for way in range(2):
+                send_a(way, s, j)
+
+        for j in range(NY):
+            pass_on(2, j)
+        for way, peer in ways_y:
+            got_b(way, 0)
+            sb[st, way, 2] = enc_b(y_c[way] + dec_b(rb[st, way, 0]))
+            send_b(way, 2, peer)
+        fill(3)
+        for j in range(NY):
+            pass_on(3, j)
+            fill(4 + j)
+        late()
+        for i in range(8, 11):
+            fill(i)
+        for way in range(2):
+            for kind in (1, 2):
+                got_b(way, kind)
+        low = y_b[0 : NZ // 2] + dec_b(rb[st, 0, 2]) + dec_b(rb[st, 1, 1])
+        y_b[0 : NZ // 2] = low
+        szb[st, 0 : NZ // 2] = enc_b(low)
+        high = y_b[NZ // 2 :] + dec_b(rb[st, 0, 1]) + dec_b(rb[st, 1, 2])
+        y_b[NZ // 2 :] = high
+        szb[st, NZ // 2 :] = enc_b(high)
+        for k in (4, 3, 5, 2, 6, 1, 7):
+            send(szb.at[st, zp[k]], rzb.at[st, k], sem_szb.at[st], sem_rzb.at[k], z=zp[k])
+        for j in range(NY):
+            for way in range(2):
+                got_a(way, 3, j)
+            total = dec_a(ra[st, 0, 3, j]) + dec_a(ra[st, 1, 3, j]) + y_a[z, j]
             y_a[z, j] = total
             sya[st, j] = enc_a(total)
         for k in (2, 1, 3):
@@ -347,11 +375,11 @@
             return gb.at[it, yy, zz, pl.ds(0, RB)]
 
         def put_a(way, s, k):
-            block = part_a(it, zm[s] if way == 0 else zp[s], ym[k])
-            send(block, block, sem_gs.at[it, 0], sem_ga.at[way, s, k], z=zp[1] if way == 0 else zm[1])
+            block = part_a(it, along_z(1 - way, s - 1 if s else 2), ym[k])
+            send(block, block, sem_gs.at[it, 0], sem_ga.at[way, s, k], z=along_z(way, 1 if s else 2))
 
         def got_a(way, s, k):
-            block = part_a(it, zm[s + 1] if way == 0 else zp[s + 1], ym[k])
+            block = part_a(it, along_z(1 - way, s if s else 4), ym[k])
             arrived(block, sem_gs.at[it, 0], sem_ga.at[way, s, k], z=zp[1])
 
         def put_b(way, s, k):
@@ -372,23 +400,25 @@
         own_a, own_b = part_a(it, z, y), part_b(it, y, z)
         for k in (2, 1, 3):
             send(own_a, own_a, sem_gs.at[it, 2], sem_gay.at[k], y=yp[k])
-        put_a(0, 0, 0)
-        put_a(1, 0, 0)
+        put_a(0, 1, 0)
+        put_a(1, 1, 0)
         for k in (5, 3, 2, 6, 1, 7):
             send(own_b, own_b, sem_gs.at[it, 3], sem_gb.at[k], z=zp[k])
         put_b(0, 0, 0)
         put_b(1, 0, 0)
         for k in (1, 3, 2):
             arrived(part_a(it, z, ym[k]), sem_gs.at[it, 2], sem_gay.at[k], y=yp[k])
-            put_a(0, 0, k)
-            put_a(1, 0, k)
+            put_a(0, 1, k)
+            put_a(1, 1, k)
         v = dot(aa[z], ga[it, z].reshape(NY * LANES, LANES))
         for s in range(1, 4):
             for k in (0, 1, 3, 2):
-                for way in (long_way(k), 1 - long_way(k)):
-                    got_a(way, s - 1, k)
-                    if s < hops(way, k):
-                        put_a(way, s, k)
+                for way in range(2):
+                    got_a(way, s, k)
+                    if s == 2 and way == long_way(k):
+                        put_a(way, 0, k)
+                    if s < 3:
+                        put_a(way, s + 1, k)
             if s == 1:
                 for k in (1, 7, 2, 6, 5, 3):
                     from_z(k)
@@ -416,7 +446,7 @@
             got_b(1, 1, k)
         v = v + dot(ab[yp[2]], gb[it, yp[2]].reshape(NZ * LANES, LANES))
         for k in range(NY):
-            got_a(long_way(k), 3, k)
+            got_a(long_way(k), 0, k)
         sent(ga.at[it, pl.ds(0, NZ - 1), :, pl.ds(0, RA)], sem_gs.at[it, 0])
         sent(gb.at[it, pl.ds(0, NY - 1), :, pl.ds(0, RB)], sem_gs.at[it, 1])
         sent(ga.at[it, 0, pl.ds(0, NY - 1), pl.ds(0, RA)], sem_gs.at[it, 2])
@@ -547,7 +577,7 @@
         vm((rows, LANES), F32),
         vm((RA, LANES), F32), vm((RB, LANES), F32), vm((RA, LANES), F32), vm((RB, LANES), F32),
         vm((4 * LANES, LANES), F32),
-        vm((2 * BAND, 4 * BAND), F32),
+        vm((2 * BAND, 4 * BAND), F32), vm((2 * BAND, 4 * BAND), BF16), vm((2 * BAND, 4 * BAND), BF16),
         vm((NZ, NY, RA, 128), F32),
         vm((NZ, RB, 128), F32),
         vm((2, NZ // 2, RB, 128), F32),

time: 155 us -> 149 us (0.961); the launches traced: 155 us -> 147 us
  Pallas kernels: 151 us -> 142 us
    pallas_call x1, Pallas kernels: 151 us -> 142 us  [shards(): pl.pallas_call(kernel, name='cg', out_shape=(out, out), in_specs=[pl.Bloc...]
where the time goes in v4:
time: 149 us; the launch traced here: 147 us
  Pallas kernels  142 us (95%)
  local copies, waits for them, and re-layouts  3.09 us (2%)
    pallas_call x1, Pallas kernels, shards(): pl.pallas_call(kernel, name='cg', out_shape=(out, out), in_specs=[pl.Bloc...  142 us
    unnamed x2, local copies, waits for them, and re-layouts  3.09 us

profile of v4, /device:TPU:1, one launch (start us, length us, event | category | flops | bytes accessed | tf_op | source)
XLA Modules:
  0.0 146.9 jit_solution(578223048064921052)
XLA Ops:
  1.3 142.5 %cg.1 = (f32[196,128]{1,0:T(8,128)}, f32[196,128]{1,0:T(8,128)}) custom-call(bf16[256,6272]{1,0:T(8,128)(2,1)} %design.1, f32[256,128]{1,0:T(8,128)} %obs.1, s32[1]{0:T(128)S(6)} %copy.11.counts, s32[2,128]{1,0:T(2,128)} %bitcast.6, f32[1,128]{1,0:T(1,128)} %bitcast.7, f32[49,128]{1,0:T(8,128)} %bitcast.4, f32[49,128]{1,0:T(8,128)} %bitcast.5), custom_call_target="tpu_custom_call" | custom-call | tf_op jit(solution)/shard_map/cg/pallas_call | solution.py:610
  143.8 1.5 %copy.12 = f32[196,128]{1,0:T(8,128)} copy(f32[196,128]{1,0:T(8,128)} %get-tuple-element.4) | data formatting | bytes 200704
  145.3 1.5 %copy.13 = f32[196,128]{1,0:T(8,128)} copy(f32[196,128]{1,0:T(8,128)} %get-tuple-element.5) | data formatting | bytes 200704

commit v5 on v4

--- a/solution.py
+++ b/solution.py
@@ -169,8 +169,13 @@
     def at_b(target):
         return atb[target].reshape(NZ * RB, 2 * BAND)
 
-    early_rows = 16
-    lax.fori_loop(0, early_rows, put_rows, 0)
+    def put_four(i, carry):
+        for k in range(4):
+            put_rows(4 * i + k, carry)
+        return carry
+
+    early_fours = 4
+    lax.fori_loop(0, early_fours, put_four, 0)
     pl.semaphore_wait(barrier, len(peers))
     for place, goal, step in ((2, 0, t_up), (1, 3, t_down)):
         send(
@@ -210,7 +215,7 @@
         part_a[...] = jnp.where(row_a < NA, column[pl.ds(shift, RA), :], 0.0)
         part_b[...] = jnp.where(row_b < NB, column[pl.ds(shift + NA, RB), :], 0.0)
 
-    lax.fori_loop(early_rows, NZ * NY, put_rows, 0)
+    lax.fori_loop(early_fours, NZ * NY // 4, put_four, 0)
 
     def filtered(st):
         ext = dec_v(hq[st])
@@ -295,7 +300,7 @@
         lax.fori_loop(0, 5, product, 0)
         y_b[...] = dot(at_b(y), w).reshape(NZ, RB, 128)
         early()
-        for i in range(3):
+        for i in range(2):
             fill(i)
 
         def pass_on(s, j):
@@ -320,12 +325,11 @@
             got_b(way, 0)
             sb[st, way, 2] = enc_b(y_c[way] + dec_b(rb[st, way, 0]))
             send_b(way, 2, peer)
-        fill(3)
+        fill(2)
         for j in range(NY):
             pass_on(3, j)
-            fill(4 + j)
         late()
-        for i in range(8, 11):
+        for i in range(3, 6):
             fill(i)
         for way in range(2):
             for kind in (1, 2):
@@ -346,6 +350,8 @@
             sya[st, j] = enc_a(total)
         for k in (2, 1, 3):
             send(sya.at[st, yp[k]], rya.at[st, k], sem_sya.at[st], sem_rya.at[k], y=yp[k])
+        for i in range(6, 11):
+            fill(i)
         sum_b = y_b[z]
         for k in range(1, NZ):
             arrived(rzb.at[st, k], sem_szb.at[st], sem_rzb.at[k], z=zp[k])
@@ -406,45 +412,61 @@
             send(own_b, own_b, sem_gs.at[it, 3], sem_gb.at[k], z=zp[k])
         put_b(0, 0, 0)
         put_b(1, 0, 0)
-        for k in (1, 3, 2):
-            arrived(part_a(it, z, ym[k]), sem_gs.at[it, 2], sem_gay.at[k], y=yp[k])
-            put_a(0, 1, k)
-            put_a(1, 1, k)
-        v = dot(aa[z], ga[it, z].reshape(NY * LANES, LANES))
-        for s in range(1, 4):
-            for k in (0, 1, 3, 2):
+        def pass_a(s, blocks):
+            for k in blocks:
                 for way in range(2):
                     got_a(way, s, k)
                     if s == 2 and way == long_way(k):
                         put_a(way, 0, k)
                     if s < 3:
                         put_a(way, s + 1, k)
-            if s == 1:
-                for k in (1, 7, 2, 6, 5, 3):
-                    from_z(k)
-            if s == 2:
-                from_z(4)
-                for k in first_half:
-                    got_b(0, 0, k)
-                    put_b(0, 1, k)
-                for k in second_half:
-                    got_b(1, 0, k)
-                    put_b(1, 1, k)
-                middle()
-            v = v + dot(aa[zm[s]], ga[it, zm[s]].reshape(NY * LANES, LANES))
-            v = v + dot(aa[zp[s]], ga[it, zp[s]].reshape(NY * LANES, LANES))
-        v = v + dot(ab[y], gb[it, y].reshape(NZ * LANES, LANES))
+
+        def pass_b(blocks):
+            for k in blocks:
+                way = 0 if k in first_half else 1
+                got_b(way, 0, k)
+                put_b(way, 1, k)
+
+        def times_a(v, zz):
+            return v + dot(aa[zz], ga[it, zz].reshape(NY * LANES, LANES))
+
+        def times_b(v, yy):
+            return v + dot(ab[yy], gb[it, yy].reshape(NZ * LANES, LANES))
+
+        for k in (1, 3, 2):
+            arrived(part_a(it, z, ym[k]), sem_gs.at[it, 2], sem_gay.at[k], y=yp[k])
+            put_a(0, 1, k)
+            put_a(1, 1, k)
+        pass_a(1, (0,))
+        pass_b((0,))
+        for k in (1, 7, 2, 6):
+            from_z(k)
+        middle()
+        for k in (5, 3):
+            from_z(k)
+        v = dot(aa[z], ga[it, z].reshape(NY * LANES, LANES))
+        pass_a(1, (1, 3, 2))
+        pass_a(2, (0,))
+        pass_b((1, 7, 2, 6))
+        v = times_a(times_a(v, zm[1]), zp[1])
+        pass_b((5, 3))
+        from_z(4)
+        pass_a(2, (1, 3, 2))
+        pass_a(3, (0,))
+        v = times_b(times_a(times_a(v, zm[2]), zp[2]), y)
+        pass_b((4,))
         for k in second_half:
             got_b(0, 0, k)
         for k in first_half:
             got_b(1, 0, k)
-        v = v + dot(ab[yp[1]], gb[it, yp[1]].reshape(NZ * LANES, LANES))
-        v = v + dot(ab[ym[1]], gb[it, ym[1]].reshape(NZ * LANES, LANES))
+        v = times_b(times_b(v, yp[1]), ym[1])
+        pass_a(3, (1, 3, 2))
+        v = times_a(times_a(v, zm[3]), zp[3])
         for k in first_half:
             got_b(0, 1, k)
         for k in second_half:
             got_b(1, 1, k)
-        v = v + dot(ab[yp[2]], gb[it, yp[2]].reshape(NZ * LANES, LANES))
+        v = times_b(v, yp[2])
         for k in range(NY):
             got_a(long_way(k), 0, k)
         sent(ga.at[it, pl.ds(0, NZ - 1), :, pl.ds(0, RA)], sem_gs.at[it, 0])

time: 149 us -> 142 us (0.953)
  Pallas kernels: 142 us -> 135 us
    pallas_call x1, Pallas kernels: 142 us -> 135 us  [shards(): pl.pallas_call(kernel, name='cg', out_shape=(out, out), in_specs=[pl.Bloc...]
where the time goes in v5:
time: 142 us; the launch traced here: 139 us
  Pallas kernels  135 us (95%)
  local copies, waits for them, and re-layouts  3.09 us (2%)
    pallas_call x1, Pallas kernels, shards(): pl.pallas_call(kernel, name='cg', out_shape=(out, out), in_specs=[pl.Bloc...  135 us
    unnamed x2, local copies, waits for them, and re-layouts  3.09 us

profile of v5, /device:TPU:1, one launch (start us, length us, event | category | flops | bytes accessed | tf_op | source)
XLA Modules:
  0.0 139.4 jit_solution(16392527278224426367)
XLA Ops:
  1.3 135.1 %cg.1 = (f32[196,128]{1,0:T(8,128)}, f32[196,128]{1,0:T(8,128)}) custom-call(bf16[256,6272]{1,0:T(8,128)(2,1)} %design.1, f32[256,128]{1,0:T(8,128)} %obs.1, s32[1]{0:T(128)S(6)} %copy.11.counts, s32[2,128]{1,0:T(2,128)} %bitcast.6, f32[1,128]{1,0:T(1,128)} %bitcast.7, f32[49,128]{1,0:T(8,128)} %bitcast.4, f32[49,128]{1,0:T(8,128)} %bitcast.5), custom_call_target="tpu_custom_call" | custom-call | tf_op jit(solution)/shard_map/cg/pallas_call | solution.py:632
  136.3 1.5 %copy.12 = f32[196,128]{1,0:T(8,128)} copy(f32[196,128]{1,0:T(8,128)} %get-tuple-element.4) | data formatting | bytes 200704
  137.9 1.5 %copy.13 = f32[196,128]{1,0:T(8,128)} copy(f32[196,128]{1,0:T(8,128)} %get-tuple-element.5) | data formatting | bytes 200704

commit v6 on v5

--- a/solution.py
+++ b/solution.py
@@ -319,12 +319,14 @@
             for way in range(2):
                 send_a(way, s, j)
 
-        for j in range(NY):
-            pass_on(2, j)
+        pass_on(2, 0)
+        pass_on(2, 1)
         for way, peer in ways_y:
             got_b(way, 0)
             sb[st, way, 2] = enc_b(y_c[way] + dec_b(rb[st, way, 0]))
             send_b(way, 2, peer)
+        pass_on(2, 2)
+        pass_on(2, 3)
         fill(2)
         for j in range(NY):
             pass_on(3, j)
@@ -353,11 +355,11 @@
         for i in range(6, 11):
             fill(i)
         sum_b = y_b[z]
-        for k in range(1, NZ):
+        for k in (1, 7, 2, 6, 3, 5, 4):
             arrived(rzb.at[st, k], sem_szb.at[st], sem_rzb.at[k], z=zp[k])
             sum_b = sum_b + dec_b(rzb[st, k])
         sum_a = y_a[z, y]
-        for k in range(1, NY):
+        for k in (1, 3, 2):
             arrived(rya.at[st, k], sem_sya.at[st], sem_rya.at[k], y=yp[k])
             sum_a = sum_a + dec_a(rya[st, k])
         for way in range(2):
@@ -490,7 +492,7 @@
         scx[it, 0] = scal
         for k in (2, 1, 3):
             send(scx.at[it, 0], scx.at[it, k], sem_us.at[it, 1], sem_uc.at[it, k], x=xp[k])
-        for k in range(1, NX):
+        for k in (1, 3, 2):
             arrived(ur.at[it, k], sem_us.at[it, 0], sem_ur.at[it, k], x=xp[k])
             chip = chip + dec_v(ur[it, k])
             arrived(scx.at[it, k], sem_us.at[it, 1], sem_uc.at[it, k], x=xp[k])

time: 142 us -> 142 us (level)
  no operation moved by 1% of the time
where the time goes in v6:
time: 142 us; the launch traced here: 140 us
  Pallas kernels  136 us (96%)
  local copies, waits for them, and re-layouts  3.09 us (2%)
    pallas_call x1, Pallas kernels, shards(): pl.pallas_call(kernel, name='cg', out_shape=(out, out), in_specs=[pl.Bloc...  136 us
    unnamed x2, local copies, waits for them, and re-layouts  3.09 us

profile of v6, /device:TPU:1, one launch (start us, length us, event | category | flops | bytes accessed | tf_op | source)
XLA Modules:
  0.0 140.0 jit_solution(8272691219579470835)
XLA Ops:
  1.3 135.6 %cg.1 = (f32[196,128]{1,0:T(8,128)}, f32[196,128]{1,0:T(8,128)}) custom-call(bf16[256,6272]{1,0:T(8,128)(2,1)} %design.1, f32[256,128]{1,0:T(8,128)} %obs.1, s32[1]{0:T(128)S(6)} %copy.11.counts, s32[2,128]{1,0:T(2,128)} %bitcast.6, f32[1,128]{1,0:T(1,128)} %bitcast.7, f32[49,128]{1,0:T(8,128)} %bitcast.4, f32[49,128]{1,0:T(8,128)} %bitcast.5), custom_call_target="tpu_custom_call" | custom-call | tf_op jit(solution)/shard_map/cg/pallas_call | solution.py:634
  136.9 1.5 %copy.12 = f32[196,128]{1,0:T(8,128)} copy(f32[196,128]{1,0:T(8,128)} %get-tuple-element.4) | data formatting | bytes 200704
  138.4 1.5 %copy.13 = f32[196,128]{1,0:T(8,128)} copy(f32[196,128]{1,0:T(8,128)} %get-tuple-element.5) | data formatting | bytes 200704
